TPU v7x, 32 devices: a whole 2x2x4 slice. The times are simulated.
32 devices in a mesh: dp: 32 (over z, y, x, core).
Axes of the slice: x: 2, y: 2, z: 4, core: 2. Of those that a mesh axis runs over, the one named last changes fastest.
Arguments:
- x_saved: bfloat16 [192, 64, 2048], P('dp')
- grad_out: bfloat16 [192, 64, 2048], P('dp')
- positions: int32 [192, 64], P('dp')
- attn_gain: bfloat16 [2048], replicated
- w_query: bfloat16 [2048, 32, 64], replicated
- w_key: bfloat16 [2048, 4, 64], replicated
- w_value: bfloat16 [2048, 4, 64], replicated
- w_out: bfloat16 [32, 64, 2048], replicated
- mlp_gain: bfloat16 [2048], replicated
- w_gate: bfloat16 [2048, 5632], replicated
- w_up: bfloat16 [2048, 5632], replicated
- w_down: bfloat16 [5632, 2048], replicated
- master_flat: float32 [44044288], P('dp')
- adam_mean: float32 [44044288], P('dp')
- adam_var: float32 [44044288], P('dp')
Outputs:
- output 1: bfloat16 [192, 64, 2048], P('dp')
- output 2: bfloat16 [2048], replicated
- output 3: bfloat16 [2048, 32, 64], replicated
- output 4: bfloat16 [2048, 4, 64], replicated
- output 5: bfloat16 [2048, 4, 64], replicated
- output 6: bfloat16 [32, 64, 2048], replicated
- output 7: bfloat16 [2048], replicated
- output 8: bfloat16 [2048, 5632], replicated
- output 9: bfloat16 [2048, 5632], replicated
- output 10: bfloat16 [5632, 2048], replicated
- output 11: float32 [44044288], P('dp')
- output 12: float32 [44044288], P('dp')
- output 13: float32 [44044288], P('dp')
- output 14: float32 [], replicated
All inputs are finite; a program needn't handle non-finite values.
Results may differ from a plain program's by a relative error of at most 0.0160587.
Values are sent between devices in bfloat16 or wider.
A program may use at most 1 GiB of HBM per device.

v0:
```python
import jax
import jax.numpy as jnp
from jax import lax
from jax.sharding import PartitionSpec as P

NORM_EPS = 1e-5
ROPE_BASE = 10000.0
LEARN_RATE = 2e-3
BETA_ONE = 0.9
BETA_TWO = 0.95
ADAM_EPS = 1e-8
WEIGHT_DECAY = 0.1
STEP_COUNT = 100


def rope_tables(positions, head_dim):
    half_dim = head_dim // 2
    inv_freq = ROPE_BASE ** (-2.0 * jnp.arange(half_dim, dtype=jnp.float32) / head_dim)
    angles = positions.astype(jnp.float32)[:, :, None] * inv_freq
    cos_full = jnp.concatenate([jnp.cos(angles), jnp.cos(angles)], axis=-1)[:, :, None, :]
    sin_full = jnp.concatenate([jnp.sin(angles), jnp.sin(angles)], axis=-1)[:, :, None, :]
    return cos_full, sin_full


def rope_apply(values, cos_full, sin_full):
    half_dim = values.shape[-1] // 2
    rotated = jnp.concatenate([-values[..., half_dim:], values[..., :half_dim]], axis=-1)
    return values * cos_full + rotated * sin_full


def rope_back(grad_rot, cos_full, sin_full):
    half_dim = grad_rot.shape[-1] // 2
    scaled = grad_rot * sin_full
    return grad_rot * cos_full + jnp.concatenate([scaled[..., half_dim:], -scaled[..., :half_dim]], axis=-1)


def rms_parts(values):
    inv_rms = lax.rsqrt(jnp.mean(values * values, axis=-1, keepdims=True) + NORM_EPS)
    return inv_rms, values * inv_rms


def rms_back(d_normed, gain_wide, inv_rms, x_hat):
    d_hat = d_normed * gain_wide
    return inv_rms * (d_hat - x_hat * jnp.mean(d_hat * x_hat, axis=-1, keepdims=True))


def local_grads(x_loc, dy_loc, pos_loc, w_list):
    attn_gain, w_query, w_key, w_value, w_out, mlp_gain, w_gate, w_up, w_down = w_list
    num_seqs, seq_len, model_dim = x_loc.shape
    num_heads, head_dim = w_query.shape[1], w_query.shape[2]
    kv_heads = w_key.shape[1]
    group_size = num_heads // kv_heads
    n_tok = num_seqs * seq_len
    wq_flat = w_query.reshape(model_dim, num_heads * head_dim)
    wk_flat = w_key.reshape(model_dim, kv_heads * head_dim)
    wv_flat = w_value.reshape(model_dim, kv_heads * head_dim)
    wo_flat = w_out.reshape(num_heads * head_dim, model_dim)
    dy_flat = dy_loc.reshape(n_tok, model_dim)
    x_wide = x_loc.reshape(n_tok, model_dim).astype(jnp.float32)
    inv_one, value_a8 = rms_parts(x_wide)
    gain_one = attn_gain.astype(jnp.float32)
    normed = (value_a8 * gain_one).astype(jnp.bfloat16)
    q_pre = jnp.dot(normed, wq_flat, preferred_element_type=jnp.float32).reshape(num_seqs, seq_len, num_heads, head_dim)
    k_pre = jnp.dot(normed, wk_flat, preferred_element_type=jnp.float32).reshape(num_seqs, seq_len, kv_heads, head_dim)
    v_heads = jnp.dot(normed, wv_flat, preferred_element_type=jnp.float32).astype(jnp.bfloat16).reshape(num_seqs, seq_len, kv_heads, head_dim)
    cos_full, sin_full = rope_tables(pos_loc, head_dim)
    q_rot = rope_apply(q_pre, cos_full, sin_full).astype(jnp.bfloat16).reshape(num_seqs, seq_len, kv_heads, group_size, head_dim)
    k_rot = rope_apply(k_pre, cos_full, sin_full).astype(jnp.bfloat16)
    score_scale = head_dim ** -0.5
    scores = jnp.einsum('bqkgd,bskd->bkgqs', q_rot, k_rot, preferred_element_type=jnp.float32) * score_scale
    causal = lax.iota(jnp.int32, seq_len)[:, None] >= lax.iota(jnp.int32, seq_len)[None, :]
    attn_probs = jax.nn.softmax(jnp.where(causal, scores, -1e30), axis=-1)
    probs_low = attn_probs.astype(jnp.bfloat16)
    context = jnp.einsum('bkgqs,bskd->bqkgd', probs_low, v_heads, preferred_element_type=jnp.float32).astype(jnp.bfloat16)
    context = context.reshape(n_tok, num_heads * head_dim)
    attn_out = jnp.dot(context, wo_flat, preferred_element_type=jnp.float32)
    hidden = (x_wide + attn_out).astype(jnp.bfloat16)
    inv_two, array_b8 = rms_parts(hidden.astype(jnp.float32))
    gain_two = mlp_gain.astype(jnp.float32)
    normed_mlp = (array_b8 * gain_two).astype(jnp.bfloat16)
    gate_pre = jnp.dot(normed_mlp, w_gate, preferred_element_type=jnp.float32)
    up_pre = jnp.dot(normed_mlp, w_up, preferred_element_type=jnp.float32)
    gate_sig = jax.nn.sigmoid(gate_pre)
    gate_act = gate_pre * gate_sig
    gated_act = (gate_act * up_pre).astype(jnp.bfloat16)
    g_down = jnp.einsum('nf,nd->fd', gated_act, dy_flat, preferred_element_type=jnp.float32)
    d_gated = jnp.einsum('nd,fd->nf', dy_flat, w_down, preferred_element_type=jnp.float32)
    d_up = (d_gated * gate_act).astype(jnp.bfloat16)
    d_gate = (d_gated * up_pre * gate_sig * (1.0 + gate_pre * (1.0 - gate_sig))).astype(jnp.bfloat16)
    g_gate = jnp.einsum('nd,nf->df', normed_mlp, d_gate, preferred_element_type=jnp.float32)
    g_up = jnp.einsum('nd,nf->df', normed_mlp, d_up, preferred_element_type=jnp.float32)
    d_normed_mlp = (jnp.einsum('nf,df->nd', d_gate, w_gate, preferred_element_type=jnp.float32)
                    + jnp.einsum('nf,df->nd', d_up, w_up, preferred_element_type=jnp.float32))
    g_mlp_gain = jnp.sum(d_normed_mlp * array_b8, axis=0)
    d_hidden = rms_back(d_normed_mlp, gain_two, inv_two, array_b8) + dy_flat.astype(jnp.float32)
    d_hidden_low = d_hidden.astype(jnp.bfloat16)
    g_out = jnp.einsum('nc,nd->cd', context, d_hidden_low, preferred_element_type=jnp.float32)
    d_context = jnp.einsum('nd,cd->nc', d_hidden_low, wo_flat, preferred_element_type=jnp.float32).astype(jnp.bfloat16)
    d_context = d_context.reshape(num_seqs, seq_len, kv_heads, group_size, head_dim)
    d_probs = jnp.einsum('bqkgd,bskd->bkgqs', d_context, v_heads, preferred_element_type=jnp.float32)
    g_values = jnp.einsum('bkgqs,bqkgd->bskd', probs_low, d_context, preferred_element_type=jnp.float32)
    d_scores = (attn_probs * (d_probs - jnp.sum(d_probs * attn_probs, axis=-1, keepdims=True)) * score_scale).astype(jnp.bfloat16)
    d_q_rot = jnp.einsum('bkgqs,bskd->bqkgd', d_scores, k_rot, preferred_element_type=jnp.float32).reshape(num_seqs, seq_len, num_heads, head_dim)
    d_k_rot = jnp.einsum('bkgqs,bqkgd->bskd', d_scores, q_rot, preferred_element_type=jnp.float32)
    d_q_pre = rope_back(d_q_rot, cos_full, sin_full).astype(jnp.bfloat16).reshape(n_tok, num_heads * head_dim)
    d_k_pre = rope_back(d_k_rot, cos_full, sin_full).astype(jnp.bfloat16).reshape(n_tok, kv_heads * head_dim)
    d_v_pre = g_values.astype(jnp.bfloat16).reshape(n_tok, kv_heads * head_dim)
    g_query = jnp.einsum('nd,nc->dc', normed, d_q_pre, preferred_element_type=jnp.float32)
    g_key = jnp.einsum('nd,nc->dc', normed, d_k_pre, preferred_element_type=jnp.float32)
    g_value = jnp.einsum('nd,nc->dc', normed, d_v_pre, preferred_element_type=jnp.float32)
    d_normed = (jnp.einsum('nc,dc->nd', d_q_pre, wq_flat, preferred_element_type=jnp.float32)
                + jnp.einsum('nc,dc->nd', d_k_pre, wk_flat, preferred_element_type=jnp.float32)
                + jnp.einsum('nc,dc->nd', d_v_pre, wv_flat, preferred_element_type=jnp.float32))
    g_attn_gain = jnp.sum(d_normed * value_a8, axis=0)
    d_x = rms_back(d_normed, gain_one, inv_one, value_a8) + d_hidden
    grad_list = [g_attn_gain, g_query, g_key, g_value, g_out, g_mlp_gain, g_gate, g_up, g_down]
    flat_grad = jnp.concatenate([w_grad.astype(jnp.bfloat16).reshape(-1) for w_grad in grad_list])
    return d_x.astype(jnp.bfloat16).reshape(num_seqs, seq_len, model_dim), flat_grad


def gain_offset(w_list):
    return w_list[0].shape[0] + w_list[1].size + w_list[2].size + w_list[3].size + w_list[4].size


def adamw_apply(grad_vec, grad_norm, master_vec, mean_vec, var_vec, first_index, model_dim, gain_two):
    clip_scale = jnp.minimum(1.0, 1.0 / (grad_norm + 1e-6))
    clipped = grad_vec * clip_scale
    new_mean = BETA_ONE * mean_vec + (1.0 - BETA_ONE) * clipped
    new_var = BETA_TWO * var_vec + (1.0 - BETA_TWO) * clipped * clipped
    mean_hat = new_mean / (1.0 - BETA_ONE ** STEP_COUNT)
    var_hat = new_var / (1.0 - BETA_TWO ** STEP_COUNT)
    flat_index = first_index + lax.iota(jnp.int32, master_vec.shape[0])
    is_gain = (flat_index < model_dim) | ((flat_index >= gain_two) & (flat_index < gain_two + model_dim))
    decays = jnp.where(is_gain, 0.0, WEIGHT_DECAY)
    new_master = master_vec - LEARN_RATE * (mean_hat / (jnp.sqrt(var_hat) + ADAM_EPS) + decays * master_vec)
    return new_master, new_mean, new_var


def split_flat(flat_vec, w_list):
    pieces = []
    offset = 0
    for weight in w_list:
        pieces.append(flat_vec[offset:offset + weight.size].reshape(weight.shape))
        offset += weight.size
    return pieces


def solution(mesh):
    dp_size = mesh.shape['dp']

    def per_device(x_loc, dy_loc, pos_loc, attn_gain, w_query, w_key, w_value, w_out, mlp_gain, w_gate, w_up, w_down, master_loc, mean_loc, var_loc):
        w_list = (attn_gain, w_query, w_key, w_value, w_out, mlp_gain, w_gate, w_up, w_down)
        grad_x, flat_grad = local_grads(x_loc, dy_loc, pos_loc, w_list)
        grad_shard = lax.psum_scatter(flat_grad, 'dp', scatter_dimension=0, tiled=True).astype(jnp.float32) / dp_size
        grad_norm = jnp.sqrt(lax.psum(jnp.sum(grad_shard * grad_shard), 'dp'))
        shard_len = master_loc.shape[0]
        shard_start = lax.axis_index('dp') * shard_len
        new_master, new_mean, new_var = adamw_apply(grad_shard, grad_norm, master_loc, mean_loc, var_loc, shard_start, attn_gain.shape[0], gain_offset(w_list))
        gathered = lax.all_gather(new_master.astype(jnp.bfloat16), 'dp', tiled=True)
        new_weights = split_flat(gathered, w_list)
        return (grad_x,) + tuple(new_weights) + (new_master, new_mean, new_var, grad_norm)

    in_specs = (P('dp'),) * 3 + (P(),) * 9 + (P('dp'),) * 3
    out_specs = (P('dp'),) + (P(),) * 9 + (P('dp'),) * 3 + (P(),)
    return jax.shard_map(per_device, mesh=mesh, in_specs=in_specs, out_specs=out_specs, check_vma=False)
```

profile of v0, /device:TPU:0, one launch (start us, length us, event | category | flops | bytes accessed | tf_op | source)
XLA Modules:
  0.0 3681.5 jit_solution(4232100256437112899)
XLA Ops:
  16.9 9.5 fusion.3
  31.0 7.1 fusion.105
  38.2 5.5 convert_bitcast_fusion.3
  43.6 5.3 copy.60
  49.0 6.1 reshape.287
  55.1 7.5 fusion.32
  62.5 16.4 fusion.92
  78.9 15.9 fusion.94
  94.8 27.0 multiply_convert_fusion.1
  121.8 16.1 fusion.106
  137.9 17.8 fusion.31
  160.7 6.9 convolution_convert_fusion.2
  171.8 5.5 copy.67
  177.3 5.6 fusion.68
  186.6 12.8 broadcast_multiply_fusion.1
  199.4 13.5 fusion.51
  212.8 22.2 convert_bitcast_fusion
  235.0 6.8 convert_bitcast_fusion.1
  241.8 18.4 convolution_convert_fusion
  260.2 17.9 convolution_convert_fusion.1
  292.7 22.1 copy.95
  328.6 5.6 convert_element_type.169
  334.1 8.5 convert_bitcast_fusion.2
  342.7 8.5 fusion.107
  351.2 9.9 copy.94
  361.0 9.9 copy.91
  371.0 44.4 %reshape.300 = bf16[11534336]{0:T(1024)(128)(2,1)} reshape(bf16[2048,5632]{1,0:T(8,128)(2,1)} %convolution_convert_fusion) | data formatting | bytes 46137344 | tf_op jit(solution)/shard_map/reshape | solution.py:117
  415.3 44.5 %reshape.299 = bf16[11534336]{0:T(1024)(128)(2,1)} reshape(bf16[2048,5632]{1,0:T(8,128)(2,1)} %convolution_convert_fusion.1) | data formatting | bytes 46137344 | tf_op jit(solution)/shard_map/reshape | solution.py:117
  459.9 5.8 fusion.41
  466.3 8.1 constant_dynamic-update-slice_fusion.7
  482.9 11.2 constant_dynamic-update-slice_fusion.2
  494.1 21.6 constant_dynamic-update-slice_fusion.1
  515.8 9.0 constant_dynamic-update-slice_fusion
  524.9 1230.2 %all-reduce.3.cloned.1.call-done = bf16[44044288]{0:T(1024)(128)(2,1)} async-done(((bf16[44044288]{0:T(1024)(128)(2,1)}), bf16[44044288]{0:T(1024)(128)(2,1)}) %all-reduce.3.cloned.1.call-update) | async-done | bytes 88088592
  1759.3 39.2 %psum.7 = f32[]{:T(128)} all-reduce(f32[]{:T(128)} %fusion.14), channel_id=1, replica_groups=mesh['dp'=32] {'dp'}, use_global_device_ids=true, to_apply=%region_11.12 | all-reduce | flops 1 | bytes 8 | tf_op jit(solution)/shard_map/psum | solution.py:155
  1799.3 14.0 fusion.96
  1813.2 32.1 reshape.309
  1850.3 873.3 %all-gather.3.cloned.1.call-done = bf16[32,1,1376384]{2,1,0:T(2,128)(2,1)} async-done(((bf16[1,1,1376384]{2,1,0:T(2,128)(2,1)}), bf16[32,1,1376384]{2,1,0:T(2,128)(2,1)}) %all-gather.3.cloned.1.call-update) | async-done | bytes 88088592 | tf_op jit(solution)/shard_map/all_gather | solution.py:159
  2723.6 491.9 %reduce.1 = bf16[32,1376384]{1,0:T(8,128)(2,1)} reduce(bf16[32,1,1376384]{2,1,0:T(2,128)(2,1)} %all-gather.3.cloned.1.call-done, bf16[]{:T(256)} %constant.69), dimensions={1}, to_apply=%all-gather.reduce_sub_computation | reduce | bytes 176177152 | tf_op jit(solution)/shard_map/all_gather | solution.py:159
  3215.4 216.9 %reshape.310 = bf16[44044288]{0:T(1024)(128)(2,1)} reshape(bf16[32,1376384]{1,0:T(8,128)(2,1)} %reduce.1) | data formatting | bytes 176177152
  3436.3 11.4 fusion.101
  3447.7 45.9 %fusion.99 = (bf16[11534336]{0:T(1024)(128)(2,1)}, bf16[11534336]{0:T(1024)(128)(2,1)}, bf16[11534336]{0:T(1024)(128)(2,1)}) fusion(bf16[44044288]{0:T(1024)(128)(2,1)} %reshape.310), kind=kLoop, calls=%fused_computation.146 | loop fusion | bytes 138412032 | tf_op jit(solution)/shard_map/slice | solution.py:143
  3502.6 34.2 slice.102
  3536.8 13.3 reshape.305
  3550.1 20.9 reshape.302
  3571.0 18.3 copy.70
  3589.3 42.0 %reshape.307 = bf16[2048,5632]{1,0:T(8,128)(2,1)} reshape(bf16[11534336]{0:T(1024)(128)(2,1)} %get-tuple-element.51) | data formatting | bytes 46137344 | tf_op jit(solution)/shard_map/reshape | solution.py:143
  3631.3 42.1 %reshape.306 = bf16[2048,5632]{1,0:T(8,128)(2,1)} reshape(bf16[11534336]{0:T(1024)(128)(2,1)} %get-tuple-element.52) | data formatting | bytes 46137344 | tf_op jit(solution)/shard_map/reshape | solution.py:143
  (154 shorter events, 86.4 us)
Async XLA Ops:
  7.2 6.5 copy-start
  7.2 1747.9 %all-reduce.3.cloned.1.call-start = ((), (), s32[]{:S(2)}) async-start(), calls=%async_computation.1 | async-start | bytes 176177152
  11.9 1.9 copy-start.27
  13.7 3.2 copy-start.17
  27.9 3.1 copy-start.7
  28.0 3.0 copy-start.11
  28.2 2.8 copy-start.25
  43.6 11.4 copy-start.2
  62.5 16.4 copy-start.15
  78.9 15.9 copy-start.13
  177.3 5.6 copy-start.4
  182.9 3.7 copy-start.12
  186.6 12.8 copy-start.26
  199.4 13.5 copy-start.14
  212.8 22.2 copy-start.6
  212.8 22.2 copy-start.19
  235.0 6.8 copy-start.16
  278.1 6.0 copy-start.8
  278.1 6.0 copy-start.21
  279.8 4.3 copy-start.23
  279.8 4.3 copy-start.22
  289.1 25.7 slice-start.14
  292.7 22.1 slice-start.15
  323.2 10.9 copy-start.18
  334.1 8.5 copy-start.20
  415.3 44.5 %copy-start.3 = (bf16[6,64,2048]{2,1,0:T(8,128)(2,1)S(1)}, bf16[6,64,2048]{2,1,0:T(8,128)(2,1)}, u32[]{:S(2)}) copy-start(bf16[6,64,2048]{2,1,0:T(8,128)(2,1)} %param.15) | copy-start | bytes 4718596
  415.3 44.5 %copy-start.24 = (bf16[384,256]{1,0:T(8,128)(2,1)S(1)}, bf16[384,256]{1,0:T(8,128)(2,1)}, u32[]{:S(2)}) copy-start(bf16[384,256]{1,0:T(8,128)(2,1)} %copy-done.23) | copy-start | bytes 589828
  415.3 44.5 %copy-start.28 = (f32[2048]{0:T(1024)S(1)}, f32[2048]{0:T(1024)}, u32[]{:S(2)}) copy-start(f32[2048]{0:T(1024)} %copy-done.27) | copy-start | bytes 24580
  415.3 44.5 %copy-start.29 = (f32[384]{0:T(512)S(1)}, f32[384]{0:T(512)}, u32[]{:S(2)}) copy-start(f32[384]{0:T(512)} %rsqrt.21) | copy-start | bytes 4612
  459.9 16.7 slice-start.12
  459.9 21.6 slice-start.6
  459.9 21.6 slice-start.7
  466.3 8.1 copy-start.10
  466.3 9.2 copy-start.9
  466.3 10.2 slice-start.13
  466.3 15.1 slice-start.8
  466.3 15.1 slice-start.9
  476.5 4.3 copy-start.30
  476.5 5.7 slice-start.10
  476.6 6.3 slice-start.11
  482.9 32.8 slice-start
  482.9 32.8 slice-start.1
  482.9 32.8 slice-start.2
  494.1 21.6 slice-start.3
  494.1 21.6 slice-start.4
  494.1 21.6 slice-start.5
  524.8 2198.8 %all-gather.3.cloned.1.call-start = ((), (), s32[]{:S(2)}) async-start(), calls=%async_computation | async-start | bytes 181682688 | tf_op jit(solution)/shard_map/all_gather | solution.py:159
  3631.3 42.1 %copy-start.1 = (bf16[2048,4,64]{0,2,1:T(8,128)(2,1)S(1)}, bf16[2048,4,64]{0,2,1:T(8,128)(2,1)}, u32[]{:S(2)}) copy-start(bf16[2048,4,64]{0,2,1:T(8,128)(2,1)} %param.21) | copy-start | bytes 3145732
  (1 other events, 1.6 us)
Sparse Core Ops, SparseCore 0:
  524.9 1230.0 all-reduce.2
  1845.5 878.0 all-gather.2
where the time goes:
time: 3690 us; the launch traced here: 3680 us
  waiting for transfers between devices  2100 us (57%)
  local copies, waits for them, and re-layouts  721 us (20%)
  other arithmetic  537 us (15%)
  matrix products  264 us (7%)
  blocking collectives  39.2 us (1%)
    unnamed x3, waiting for transfers between devices  1230 us
    all_gather x1, waiting for transfers between devices, per_device(): gathered = lax.all_gather(new_master.astype(jnp.bfloat16), 'dp', tiled=True)  873 us
    all_gather x1, other arithmetic, per_device(): gathered = lax.all_gather(new_master.astype(jnp.bfloat16), 'dp', tiled=True)  492 us
    unnamed x112, local copies, waits for them, and re-layouts  370 us
    reshape x6, local copies, waits for them, and re-layouts, split_flat(): pieces.append(flat_vec[offset:offset + weight.size].reshape(weight.shape))  123 us
    slice x5, local copies, waits for them, and re-layouts, split_flat(): pieces.append(flat_vec[offset:offset + weight.size].reshape(weight.shape))  95.5 us
    reshape x2, local copies, waits for them, and re-layouts, local_grads(): w_grad.astype(jnp.bfloat16).reshape(-1)  88.9 us
  transfers between devices with their start and end apart: 2, of which 2 were waited for; matrix products, arithmetic and copies ran while one was open for 0% of the time, Pallas kernels for 0%

commit v1 on v0

--- a/solution.py
+++ b/solution.py
@@ -1,6 +1,10 @@
+import functools
 import jax
 import jax.numpy as jnp
+import numpy as np
 from jax import lax
+from jax.experimental import pallas as pl
+from jax.experimental.pallas import tpu as pltpu
 from jax.sharding import PartitionSpec as P
 
 NORM_EPS = 1e-5
@@ -11,6 +15,474 @@
 ADAM_EPS = 1e-8
 WEIGHT_DECAY = 0.1
 STEP_COUNT = 100
+
+MATS = ((2, 1), (4096, 16), (512, 2), (512, 2), (4096, 16), (2, 1), (11264, 44), (11264, 44), (11264, 16))
+OFFS = tuple(int(o) for o in np.cumsum([0] + [m[0] for m in MATS]))
+NDEV = 32
+TILES = OFFS[-1]
+ROWS = TILES * 8 // NDEV
+HALO = 352
+WIN_R = 1408
+WIN_A = 1376
+HALF = WIN_A // 2
+S_ROWS = 11464
+X_ROWS = 11112
+
+
+def group_of(row):
+    tile = row // 8
+    mat = max(m for m in range(len(MATS)) if OFFS[m] <= tile)
+    per = MATS[mat][1]
+    return OFFS[mat] + (tile - OFFS[mat]) // per * per, per
+
+
+def plan():
+    lo, hi, own = [], [], []
+    for dev in range(NDEV):
+        start, per = group_of(ROWS * dev)
+        last, last_per = group_of(ROWS * (dev + 1) - 1)
+        lo.append(start)
+        hi.append(last + last_per)
+        own.append(start if start * 8 == ROWS * dev else start + per)
+    own.append(TILES)
+    return lo, hi, own
+
+
+LO, HI, OWN = plan()
+BASE = [min(a, TILES - WIN_R) for a in LO]
+
+
+def overlap(a, b, mat):
+    return max(a, OFFS[mat]), min(b, OFFS[mat + 1])
+
+
+def tables():
+    rows_in, rows_out = [], []
+    for dev in range(NDEV):
+        r_in, r_out = [], []
+        for mat, (_, per) in enumerate(MATS):
+            a, b = overlap(LO[dev], HI[dev], mat)
+            n = max(0, b - a) // per
+            r_in += [a - BASE[dev], 8 * a - ROWS * dev + HALO, n] if n else [0, 0, 0]
+            a, b = overlap(OWN[dev], OWN[dev + 1], mat)
+            n = max(0, b - a) // per
+            r_out += [a - OWN[dev], 8 * a - ROWS * dev, n] if n else [0, 0, 0]
+        rows_in.append(r_in)
+        rows_out.append(r_out)
+    return np.array(rows_in, np.int32), np.array(rows_out, np.int32)
+
+
+def to_tiles(mat2d):
+    rows, cols = mat2d.shape
+    return mat2d.reshape(rows // 8, 8, cols // 128, 128).transpose(0, 2, 1, 3).reshape(-1, 8, 128)
+
+
+def from_tiles(tiles, rows, cols):
+    return tiles.reshape(rows // 8, cols // 128, 8, 128).transpose(0, 2, 1, 3).reshape(rows, cols)
+
+
+def unpermute_kernel(tab, x_ref, o_ref):
+    o_ref[0:HALO, :] = jnp.zeros((HALO, 128), jnp.float32)
+    o_ref[S_ROWS - 376:S_ROWS, :] = jnp.zeros((376, 128), jnp.float32)
+    for mat, (_, per) in enumerate(MATS):
+        t0, r0 = tab[3 * mat], tab[3 * mat + 1]
+
+        def body(g, carry, per=per, t0=t0, r0=r0):
+            for j in range(per):
+                o_ref[pl.ds(r0 + g * (8 * per) + j, 8, stride=per), :] = x_ref[t0 + g * per + j].astype(jnp.float32)
+            return carry
+
+        lax.fori_loop(0, tab[3 * mat + 2], body, 0)
+
+
+def unpermute(tab, win):
+    return pl.pallas_call(
+        unpermute_kernel,
+        out_shape=jax.ShapeDtypeStruct((S_ROWS, 128), jnp.float32),
+        grid_spec=pltpu.PrefetchScalarGridSpec(
+            num_scalar_prefetch=1, grid=(1,),
+            in_specs=[pl.BlockSpec((WIN_R, 8, 128), lambda i, t: (0, 0, 0))],
+            out_specs=pl.BlockSpec((S_ROWS, 128), lambda i, t: (0, 0))),
+        compiler_params=pltpu.CompilerParams(vmem_limit_bytes=40 << 20),
+        cost_estimate=pl.CostEstimate(flops=4000000, bytes_accessed=9000000, transcendentals=0),
+    )(tab, win)
+
+
+def permute_kernel(tab, x_ref, h_ref, o_ref, s_ref):
+    def fill(k, carry):
+        at = pl.ds(pl.multiple_of(k * 64, 64), 64)
+        s_ref[at, :] = x_ref[at, :]
+        return carry
+
+    lax.fori_loop(0, ROWS // 64, fill, 0)
+    s_ref[ROWS // 64 * 64:ROWS, :] = x_ref[ROWS // 64 * 64:ROWS, :]
+    s_ref[ROWS:ROWS + HALO, :] = h_ref[...]
+    for mat, (_, per) in enumerate(MATS):
+        t0, r0 = tab[3 * mat], tab[3 * mat + 1]
+
+        def body(g, carry, per=per, t0=t0, r0=r0):
+            for j in range(per):
+                o_ref[t0 + g * per + j] = s_ref[pl.ds(r0 + g * (8 * per) + j, 8, stride=per), :].astype(jnp.bfloat16)
+            return carry
+
+        lax.fori_loop(0, tab[3 * mat + 2], body, 0)
+
+
+def permute(tab, rows, halo):
+    return pl.pallas_call(
+        permute_kernel,
+        out_shape=jax.ShapeDtypeStruct((WIN_A, 8, 128), jnp.bfloat16),
+        grid_spec=pltpu.PrefetchScalarGridSpec(
+            num_scalar_prefetch=1, grid=(1,),
+            in_specs=[pl.BlockSpec((ROWS, 128), lambda i, t: (0, 0)), pl.BlockSpec((HALO, 128), lambda i, t: (0, 0))],
+            out_specs=pl.BlockSpec((WIN_A, 8, 128), lambda i, t: (0, 0, 0)),
+            scratch_shapes=[pltpu.VMEM((X_ROWS, 128), jnp.float32)]),
+        compiler_params=pltpu.CompilerParams(vmem_limit_bytes=40 << 20),
+        cost_estimate=pl.CostEstimate(flops=4000000, bytes_accessed=9000000, transcendentals=0),
+    )(tab, rows, halo)
+
+
+def gather_kernel(x_ref, out_ref, own_sem, send_sem, recv_sem):
+    me = lax.axis_index('dp')
+    core, xx, yy, zz = me % 2, (me // 2) % 2, (me // 4) % 2, me // 8
+
+    def dev(z, y, x, c):
+        return ((z * 2 + y) * 2 + x) * 2 + c
+
+    up, down = dev(zz + 1, yy, xx, core), dev(zz - 1, yy, xx, core)
+    xn, yn, mate = dev(zz, yy, 1 - xx, core), dev(zz, 1 - yy, xx, core), dev(zz, yy, xx, 1 - core)
+    has_up, has_down = zz < 3, zz > 0
+
+    barrier = pltpu.get_barrier_semaphore()
+    for target in (xn, yn, mate):
+        pl.semaphore_signal(barrier, inc=1, device_id=(target,), device_id_type=pl.DeviceIdType.MESH)
+    for cond, target in ((has_up, up), (has_down, down)):
+        @pl.when(cond)
+        def _(target=target):
+            pl.semaphore_signal(barrier, inc=1, device_id=(target,), device_id_type=pl.DeviceIdType.MESH)
+    pl.semaphore_wait(barrier, 3 + has_up.astype(jnp.int32) + has_down.astype(jnp.int32))
+
+    sent = []
+
+    def part(ref, h):
+        return ref.at[pl.ds(h * HALF, HALF)]
+
+    def copy(src, slot, h, target, k):
+        return pltpu.make_async_remote_copy(
+            src_ref=src, dst_ref=out_ref.at[slot, pl.ds(h * HALF, HALF)],
+            send_sem=send_sem.at[k], recv_sem=recv_sem.at[slot, h],
+            device_id=(target,), device_id_type=pl.DeviceIdType.MESH)
+
+    def send(conds, src, slot, h, target):
+        k = len(sent)
+        desc = copy(src, slot, h, target, k)
+        sent.append(conds)
+        if conds[-1] is None:
+            desc.start()
+        else:
+            @pl.when(conds[-1])
+            def _():
+                desc.start()
+
+    def arrived(slot, h):
+        copy(part(out_ref.at[slot], h), slot, h, mate, 0).wait_recv()
+
+    own_copy = pltpu.make_async_copy(x_ref, out_ref.at[me], own_sem)
+    own_copy.start()
+    for h in range(2):
+        src = part(x_ref, h)
+        send((has_up,), src, me, h, up)
+        send((has_down,), src, me, h, down)
+        send((None,), src, me, h, xn)
+        send((None,), src, me, h, yn)
+    for h in range(2):
+        send((None,), part(x_ref, h), me, h, mate)
+
+    def column(step):
+        if step == 0:
+            return [(None, zz, None)]
+        return [(zz - step >= 0, zz - step, 'up'), (zz + step <= 3, zz + step, 'down')]
+
+    def guarded(cond, body):
+        if cond is None:
+            body()
+        else:
+            pl.when(cond)(body)
+
+    for step in range(6):
+        if 1 <= step <= 3:
+            for cond, zs, way in column(step):
+                def body(cond=cond, zs=zs, way=way):
+                    slot = dev(zs, yy, xx, core)
+                    for h in range(2):
+                        arrived(slot, h)
+                        src = part(out_ref.at[slot], h)
+                        onward = has_up if way == 'up' else has_down
+                        send((cond, onward), src, slot, h, up if way == 'up' else down)
+                        send((cond, None), src, slot, h, xn)
+                        send((cond, None), src, slot, h, yn)
+                        send((cond, None), src, slot, h, mate)
+                guarded(cond, body)
+        if 1 <= step <= 4:
+            for cond, zs, _ in column(step - 1):
+                def body(cond=cond, zs=zs):
+                    for h in range(2):
+                        for side in range(2):
+                            slot = dev(zs, yy, 1 - xx, core) if side == 0 else dev(zs, 1 - yy, xx, core)
+                            arrived(slot, h)
+                            src = part(out_ref.at[slot], h)
+                            if h == side:
+                                send((cond, None), src, slot, h, yn if side == 0 else xn)
+                            send((cond, None), src, slot, h, mate)
+                guarded(cond, body)
+        if 2 <= step <= 5:
+            for cond, zs, _ in column(step - 2):
+                def body(cond=cond, zs=zs):
+                    slot = dev(zs, 1 - yy, 1 - xx, core)
+                    for h in range(2):
+                        arrived(slot, h)
+                        send((cond, None), part(out_ref.at[slot], h), slot, h, mate)
+                guarded(cond, body)
+
+    def drain(k, carry):
+        slot = (k // 2) * 2 + (1 - core)
+        out = out_ref.at[slot]
+        for h in range(2):
+            @pl.when(k % 2 == h)
+            def _(h=h):
+                arrived(slot, h)
+        return carry
+
+    lax.fori_loop(0, NDEV, drain, 0)
+    for k, conds in enumerate(sent):
+        conds = [c for c in conds if c is not None]
+        wait_send = copy(part(x_ref, 0), me, 0, mate, k).wait_send
+        if not conds:
+            wait_send()
+        else:
+            cond = conds[0]
+            for c in conds[1:]:
+                cond = jnp.logical_and(cond, c)
+            pl.when(cond)(wait_send)
+    own_copy.wait()
+
+
+def gather(shard):
+    return pl.pallas_call(
+        gather_kernel,
+        out_shape=jax.ShapeDtypeStruct((NDEV, WIN_A, 8, 128), jnp.bfloat16),
+        in_specs=[pl.BlockSpec(memory_space=pltpu.VMEM)],
+        out_specs=pl.BlockSpec(memory_space=pl.ANY),
+        scratch_shapes=[pltpu.SemaphoreType.DMA, pltpu.SemaphoreType.DMA((128,)), pltpu.SemaphoreType.DMA((NDEV, 2))],
+        compiler_params=pltpu.CompilerParams(collective_id=1, has_side_effects=True, vmem_limit_bytes=16 << 20),
+    )(shard)
+
+
+HALF_R = WIN_R // 2
+PIECES = ((1, 1, 0), (1, 1, 1), (1, 0, 0), (0, 1, 1), (0, 1, 0), (1, 0, 1), (0, 0, 0), (0, 0, 1))
+
+
+def scatter_kernel(src_ref, out_ref, land_mate, land_one, land_two, land_z, acc, tmp,
+                   load_sem, tmp_sem, out_sem, send_sem, mate_sem, one_sem, two_sem, z_sem):
+    me = lax.axis_index('dp')
+    core, xx, yy, zz = me % 2, (me // 2) % 2, (me // 4) % 2, me // 8
+
+    def dev(z, y, x, c):
+        return ((z * 2 + y) * 2 + x) * 2 + c
+
+    xn, yn, mate = dev(zz, yy, 1 - xx, core), dev(zz, 1 - yy, xx, core), dev(zz, yy, xx, 1 - core)
+    up, down = dev(zz + 1, yy, xx, core), dev(zz - 1, yy, xx, core)
+    has_up, has_down = zz < 3, zz > 0
+
+    barrier = pltpu.get_barrier_semaphore()
+    for target in (xn, yn, mate):
+        pl.semaphore_signal(barrier, inc=1, device_id=(target,), device_id_type=pl.DeviceIdType.MESH)
+    for cond, target in ((has_up, up), (has_down, down)):
+        @pl.when(cond)
+        def _(target=target):
+            pl.semaphore_signal(barrier, inc=1, device_id=(target,), device_id_type=pl.DeviceIdType.MESH)
+    pl.semaphore_wait(barrier, 3 + has_up.astype(jnp.int32) + has_down.astype(jnp.int32))
+
+    low = jnp.minimum(zz, 3 - zz)
+    flip = zz >= 2
+    order = []
+    for far, near in ((3, 3), (2, 0), (1, 2)):
+        at = jnp.where(low == 0, far, near)
+        order.append(jnp.where(flip, 3 - at, at))
+    order.append(zz)
+
+    def remote(src, dst, send, recv, target):
+        return pltpu.make_async_remote_copy(src_ref=src, dst_ref=dst, send_sem=send, recv_sem=recv,
+                                            device_id=(target,), device_id_type=pl.DeviceIdType.MESH)
+
+    def slot_half(k, piece, c):
+        dy, dx, h = piece
+        y = 1 - yy if dy else yy
+        x = 1 - xx if dx else xx
+        return src_ref.at[dev(order[k], y, x, c), pl.ds(h * HALF_R, HALF_R)]
+
+    def index(k, piece):
+        return k * 8 + PIECES.index(piece)
+
+    def to_mate(k, piece):
+        i = index(k, piece)
+        return remote(slot_half(k, piece, 1 - core), land_mate.at[i], send_sem.at[i], mate_sem.at[i], mate)
+
+    def load(k, piece):
+        i = index(k, piece)
+        return pltpu.make_async_copy(slot_half(k, piece, core), acc.at[i], load_sem.at[i])
+
+    def hop_one(k, piece):
+        j = k * 4 + (piece[1] if piece[2] == 0 else 2 + piece[0])
+        return remote(acc.at[index(k, piece)], land_one.at[j], send_sem.at[32 + j], one_sem.at[j],
+                      yn if piece[2] == 0 else xn)
+
+    def hop_two(k, h):
+        j = k * 2 + h
+        piece = (0, 1, 0) if h == 0 else (1, 0, 1)
+        return remote(acc.at[index(k, piece)], land_two.at[j], send_sem.at[48 + j], two_sem.at[j],
+                      xn if h == 0 else yn)
+
+    def hop_z(k, h, way):
+        i = index(k, (0, 0, h))
+        return remote(acc.at[i], land_z.at[way, order[k], h], send_sem.at[56 + k * 2 + h], z_sem.at[way, order[k], h],
+                      down if way else up)
+
+    def add(i, landed):
+        copy = pltpu.make_async_copy(landed, tmp, tmp_sem)
+        copy.start()
+        copy.wait()
+
+        def body(t, carry):
+            at = pl.ds(pl.multiple_of(t * 16, 16), 16)
+            acc[i, at] = (acc[i, at].astype(jnp.float32) + tmp[at].astype(jnp.float32)).astype(jnp.bfloat16)
+            return carry
+
+        lax.fori_loop(0, HALF_R // 16, body, 0)
+
+    for k in range(4):
+        for piece in PIECES:
+            to_mate(k, piece).start()
+            load(k, piece).start()
+
+    def prepare(k):
+        for piece in PIECES:
+            i = index(k, piece)
+            load(k, piece).wait()
+            to_mate(k, piece).wait_recv()
+            add(i, land_mate.at[i])
+            if piece[piece[2]] == 1:
+                hop_one(k, piece).start()
+
+    def second(k):
+        for h, piece in ((0, (0, 1, 0)), (1, (1, 0, 1))):
+            j = k * 4 + (1 if h == 0 else 3)
+            remote(tmp, land_one.at[j], send_sem.at[32 + j], one_sem.at[j], xn).wait_recv()
+            add(index(k, piece), land_one.at[j])
+            hop_two(k, h).start()
+
+    def final(k):
+        zs = order[k]
+        for h in range(2):
+            i = index(k, (0, 0, h))
+            j = k * 4 + (0 if h == 0 else 2)
+            remote(tmp, land_one.at[j], send_sem.at[32 + j], one_sem.at[j], xn).wait_recv()
+            add(i, land_one.at[j])
+        for h in range(2):
+            i = index(k, (0, 0, h))
+            hop_two(k, h).wait_recv()
+            add(i, land_two.at[k * 2 + h])
+            for way, cond in ((0, (zs >= zz) & has_down), (1, (zs <= zz) & has_up)):
+                @pl.when(cond)
+                def _(way=way, h=h, i=i):
+                    hop_z(k, h, way).wait_recv()
+                    add(i, land_z.at[way, zs, h])
+            if k < 3:
+                for way, cond in ((0, zs > zz), (1, zs < zz)):
+                    @pl.when(cond)
+                    def _(way=way, h=h):
+                        hop_z(k, h, way).start()
+            else:
+                pltpu.make_async_copy(acc.at[i], out_ref.at[pl.ds(h * HALF_R, HALF_R)], out_sem.at[h]).start()
+
+    prepare(0)
+    prepare(1)
+    second(0)
+    prepare(2)
+    second(1)
+    prepare(3)
+    final(0)
+    second(2)
+    final(1)
+    second(3)
+    final(2)
+    final(3)
+    for n in range(62):
+        remote(tmp, land_mate.at[0], send_sem.at[n], mate_sem.at[0], mate).wait_send()
+    for h in range(2):
+        pltpu.make_async_copy(acc.at[index(3, (0, 0, h))], out_ref.at[pl.ds(h * HALF_R, HALF_R)], out_sem.at[h]).wait()
+
+
+def scatter(slots):
+    def lands(*lead):
+        return jax.ShapeDtypeStruct(lead + (HALF_R, 8, 128), jnp.bfloat16)
+
+    any_spec = pl.BlockSpec(memory_space=pl.ANY)
+    dma = pltpu.SemaphoreType.DMA
+    return pl.pallas_call(
+        scatter_kernel,
+        out_shape=(jax.ShapeDtypeStruct((WIN_R, 8, 128), jnp.bfloat16), lands(32), lands(16), lands(8), lands(2, 4, 2)),
+        in_specs=[any_spec],
+        out_specs=(any_spec,) * 5,
+        scratch_shapes=[pltpu.VMEM((32, HALF_R, 8, 128), jnp.bfloat16), pltpu.VMEM((HALF_R, 8, 128), jnp.bfloat16),
+                        dma((32,)), dma, dma((2,)), dma((62,)), dma((32,)), dma((16,)), dma((8,)), dma((2, 4, 2))],
+        compiler_params=pltpu.CompilerParams(collective_id=2, has_side_effects=True, vmem_limit_bytes=56 << 20),
+    )(slots)[0]
+
+
+BUFS = 6
+
+
+def move_kernel(moves, n_in, n_out, *refs):
+    ins, outs = refs[:n_in], refs[n_in:n_in + n_out]
+    buf, in_sem, out_sem = refs[n_in + n_out:]
+
+    def read(n):
+        src, a, _, _, count = moves[n]
+        return pltpu.make_async_copy(ins[src].at[pl.ds(a, count)], buf.at[n % BUFS, pl.ds(0, count)], in_sem.at[n % BUFS])
+
+    def write(n):
+        _, _, dst, b, count = moves[n]
+        return pltpu.make_async_copy(buf.at[n % BUFS, pl.ds(0, count)], outs[dst].at[pl.ds(b, count)], out_sem.at[n % BUFS])
+
+    ahead = BUFS // 2
+    for n in range(len(moves) + ahead):
+        if n < len(moves):
+            if n >= BUFS:
+                write(n - BUFS).wait()
+            read(n).start()
+        if n >= ahead:
+            read(n - ahead).wait()
+            write(n - ahead).start()
+    for n in range(max(0, len(moves) - BUFS), len(moves)):
+        write(n).wait()
+
+
+def move(moves, arrays, out_tiles):
+    moves = tuple(m[:1] + (m[1] + c,) + m[2:3] + (m[3] + c, min(BLOCK, m[4] - c)) for m in moves for c in range(0, m[4], BLOCK))
+    return pl.pallas_call(
+        functools.partial(move_kernel, moves, len(arrays), len(out_tiles)),
+        out_shape=tuple(jax.ShapeDtypeStruct((n, 8, 128), jnp.bfloat16) for n in out_tiles),
+        in_specs=[pl.BlockSpec(memory_space=pl.ANY)] * len(arrays),
+        out_specs=(pl.BlockSpec(memory_space=pl.ANY),) * len(out_tiles),
+        scratch_shapes=[pltpu.VMEM((BUFS, BLOCK, 8, 128), jnp.bfloat16), pltpu.SemaphoreType.DMA((BUFS,)),
+                        pltpu.SemaphoreType.DMA((BUFS,))],
+        compiler_params=pltpu.CompilerParams(vmem_limit_bytes=20 << 20),
+        cost_estimate=pl.CostEstimate(flops=100000000, bytes_accessed=176000000, transcendentals=0),
+    )(*arrays)
+
+
+BLOCK = 704
 
 
 def rope_tables(positions, head_dim):
@@ -114,51 +586,82 @@
     g_attn_gain = jnp.sum(d_normed * value_a8, axis=0)
     d_x = rms_back(d_normed, gain_one, inv_one, value_a8) + d_hidden
     grad_list = [g_attn_gain, g_query, g_key, g_value, g_out, g_mlp_gain, g_gate, g_up, g_down]
-    flat_grad = jnp.concatenate([w_grad.astype(jnp.bfloat16).reshape(-1) for w_grad in grad_list])
-    return d_x.astype(jnp.bfloat16).reshape(num_seqs, seq_len, model_dim), flat_grad
-
-
-def gain_offset(w_list):
-    return w_list[0].shape[0] + w_list[1].size + w_list[2].size + w_list[3].size + w_list[4].size
-
-
-def adamw_apply(grad_vec, grad_norm, master_vec, mean_vec, var_vec, first_index, model_dim, gain_two):
-    clip_scale = jnp.minimum(1.0, 1.0 / (grad_norm + 1e-6))
-    clipped = grad_vec * clip_scale
-    new_mean = BETA_ONE * mean_vec + (1.0 - BETA_ONE) * clipped
-    new_var = BETA_TWO * var_vec + (1.0 - BETA_TWO) * clipped * clipped
+    return d_x.astype(jnp.bfloat16).reshape(num_seqs, seq_len, model_dim), grad_list
+
+
+def windows(grad_list):
+    tiles = [g.astype(jnp.bfloat16).reshape(2, 8, 128) if g.ndim == 1 else to_tiles(g.astype(jnp.bfloat16)) for g in grad_list]
+    moves = []
+    for dev in range(NDEV):
+        for mat in range(len(MATS)):
+            a, b = overlap(BASE[dev], BASE[dev] + WIN_R, mat)
+            if b > a:
+                moves.append((mat, a - OFFS[mat], 0, dev * WIN_R + a - BASE[dev], b - a))
+    return move(moves, tiles, (NDEV * WIN_R,))[0].reshape(NDEV, WIN_R, 8, 128)
+
+
+def assemble(slots, w_list):
+    moves = []
+    for dev in range(NDEV):
+        for mat in range(len(MATS)):
+            a, b = overlap(OWN[dev], OWN[dev + 1], mat)
+            if b > a:
+                moves.append((0, dev * WIN_A + a - OWN[dev], mat, a - OFFS[mat], b - a))
+    tiles = move(moves, [slots.reshape(NDEV * WIN_A, 8, 128)], tuple(m[0] for m in MATS))
+    out = []
+    for mat, weight in enumerate(w_list):
+        if weight.ndim == 1:
+            out.append(tiles[mat].reshape(weight.shape))
+        else:
+            cols = MATS[mat][1] * 128
+            out.append(from_tiles(tiles[mat], weight.size // cols, cols).reshape(weight.shape))
+    return out
+
+
+def reduce_scatter(grad_list):
+    return scatter(windows(grad_list))
+
+
+def adamw(grad, clip_scale, master, mean, var, first_row):
+    clipped = grad * clip_scale
+    new_mean = BETA_ONE * mean + (1.0 - BETA_ONE) * clipped
+    new_var = BETA_TWO * var + (1.0 - BETA_TWO) * clipped * clipped
     mean_hat = new_mean / (1.0 - BETA_ONE ** STEP_COUNT)
     var_hat = new_var / (1.0 - BETA_TWO ** STEP_COUNT)
-    flat_index = first_index + lax.iota(jnp.int32, master_vec.shape[0])
-    is_gain = (flat_index < model_dim) | ((flat_index >= gain_two) & (flat_index < gain_two + model_dim))
+    row = first_row + lax.broadcasted_iota(jnp.int32, master.shape, 0)
+    gain_two = OFFS[5] * 8
+    is_gain = (row < 16) | ((row >= gain_two) & (row < gain_two + 16))
     decays = jnp.where(is_gain, 0.0, WEIGHT_DECAY)
-    new_master = master_vec - LEARN_RATE * (mean_hat / (jnp.sqrt(var_hat) + ADAM_EPS) + decays * master_vec)
+    new_master = master - LEARN_RATE * (mean_hat / (jnp.sqrt(var_hat) + ADAM_EPS) + decays * master)
     return new_master, new_mean, new_var
 
 
-def split_flat(flat_vec, w_list):
-    pieces = []
-    offset = 0
-    for weight in w_list:
-        pieces.append(flat_vec[offset:offset + weight.size].reshape(weight.shape))
-        offset += weight.size
-    return pieces
+def update(win, master, mean, var, tab_in, tab_out):
+    me = lax.axis_index('dp')
+    state = [s.reshape(ROWS, 128) for s in (master, mean, var)]
+    edge = jnp.stack([s[:HALO] for s in state])
+    edge = lax.ppermute(edge, 'dp', [(d, d - 1) for d in range(1, NDEV)])
+    summed = unpermute(jnp.asarray(tab_in)[me], win)
+    grad = summed[HALO:HALO + ROWS] * (1.0 / NDEV)
+    grad_edge = summed[HALO + ROWS:2 * HALO + ROWS] * (1.0 / NDEV)
+    grad_norm = jnp.sqrt(lax.psum(jnp.sum(grad * grad), 'dp'))
+    clip_scale = jnp.minimum(1.0, 1.0 / (grad_norm + 1e-6))
+    new_state = adamw(grad, clip_scale, *state, me * ROWS)
+    edge_master = adamw(grad_edge, clip_scale, edge[0], edge[1], edge[2], (me + 1) * ROWS)[0]
+    shard = permute(jnp.asarray(tab_out)[me], new_state[0], edge_master)
+    return [s.reshape(-1) for s in new_state], grad_norm, shard
 
 
 def solution(mesh):
-    dp_size = mesh.shape['dp']
+    tab_in, tab_out = tables()
 
     def per_device(x_loc, dy_loc, pos_loc, attn_gain, w_query, w_key, w_value, w_out, mlp_gain, w_gate, w_up, w_down, master_loc, mean_loc, var_loc):
         w_list = (attn_gain, w_query, w_key, w_value, w_out, mlp_gain, w_gate, w_up, w_down)
-        grad_x, flat_grad = local_grads(x_loc, dy_loc, pos_loc, w_list)
-        grad_shard = lax.psum_scatter(flat_grad, 'dp', scatter_dimension=0, tiled=True).astype(jnp.float32) / dp_size
-        grad_norm = jnp.sqrt(lax.psum(jnp.sum(grad_shard * grad_shard), 'dp'))
-        shard_len = master_loc.shape[0]
-        shard_start = lax.axis_index('dp') * shard_len
-        new_master, new_mean, new_var = adamw_apply(grad_shard, grad_norm, master_loc, mean_loc, var_loc, shard_start, attn_gain.shape[0], gain_offset(w_list))
-        gathered = lax.all_gather(new_master.astype(jnp.bfloat16), 'dp', tiled=True)
-        new_weights = split_flat(gathered, w_list)
-        return (grad_x,) + tuple(new_weights) + (new_master, new_mean, new_var, grad_norm)
+        grad_x, grad_list = local_grads(x_loc, dy_loc, pos_loc, w_list)
+        win = reduce_scatter(grad_list)
+        new_state, grad_norm, shard = update(win, master_loc, mean_loc, var_loc, tab_in, tab_out)
+        new_weights = assemble(gather(shard), w_list)
+        return (grad_x,) + tuple(new_weights) + tuple(new_state) + (grad_norm,)
 
     in_specs = (P('dp'),) * 3 + (P(),) * 9 + (P('dp'),) * 3
     out_specs = (P('dp'),) + (P(),) * 9 + (P('dp'),) * 3 + (P(),)

time: 3690 us -> 1410 us (0.38)
  waiting for transfers between devices: 2100 us -> 0.01 us
  Pallas kernels: 0 us -> 919 us
  local copies, waits for them, and re-layouts: 721 us -> 120 us
  other arithmetic: 537 us -> 44.4 us
    unnamed x3 -> x0, waiting for transfers between devices: 1230 us -> none
    pallas_call x0 -> x6, Pallas kernels: none -> 919 us  [the longest x1 429 us: scatter(): pl.pallas_call(scatter_kernel, out_shape=(jax.ShapeDtypeStruct((WIN_R, 8,...]
    all_gather x1 -> x0, waiting for transfers between devices: 873 us -> none  [per_device(): gathered = lax.all_gather(new_master.astype(jnp.bfloat16), 'dp', tiled=True)]
    all_gather x1 -> x0, other arithmetic: 492 us -> none  [per_device(): gathered = lax.all_gather(new_master.astype(jnp.bfloat16), 'dp', tiled=True)]
    unnamed x112 -> x75, local copies, waits for them, and re-layouts: 370 us -> 38.8 us
    reshape x8 -> x3, local copies, waits for them, and re-layouts: 211 us -> 13.9 us  [from_tiles(): tiles.reshape(rows // 8, cols // 128, 8, 128).transpose(0, 2, 1, 3)]
    slice x5 -> x0, local copies, waits for them, and re-layouts: 95.5 us -> none  [split_flat(): pieces.append(flat_vec[offset:offset + weight.size].reshape(weight.shape))]
  transfers between devices with their start and end apart: 2 -> 1, of which waited for: 2 -> 0; matrix products, arithmetic and copies ran while one was open for 0% -> 25% of each run, Pallas kernels for 0% -> 35%
where the time goes in v1:
time: 1410 us; the launch traced here: 1400 us
  Pallas kernels  919 us (65%)
  matrix products  270 us (19%)
  local copies, waits for them, and re-layouts  120 us (9%)
  blocking collectives  46 us (3%)
  other arithmetic  44.4 us (3%)
    pallas_call x1, Pallas kernels, scatter(): pl.pallas_call(scatter_kernel, out_shape=(jax.ShapeDtypeStruct((WIN_R, 8,...  429 us
    pallas_call x1, Pallas kernels, gather(): pl.pallas_call(gather_kernel, out_shape=jax.ShapeDtypeStruct((NDEV, WIN_A...  373 us
    pallas_call x2, Pallas kernels, move(): pl.pallas_call(functools.partial(move_kernel, moves, len(arrays), len(out...  110 us
    psum x1, blocking collectives, update(): grad_norm = jnp.sqrt(lax.psum(jnp.sum(grad * grad), 'dp'))  46 us
    unnamed x75, local copies, waits for them, and re-layouts  38.8 us
    another operation x3, local copies, waits for them, and re-layouts, assemble(): from_tiles(tiles[mat], weight.size // cols, cols).reshape(weight.shape)  30.7 us
  transfers between devices with their start and end apart: 1, of which 0 were waited for; matrix products, arithmetic and copies ran while one was open for 25% of the time, Pallas kernels for 35%

profile of v1, /device:TPU:0, one launch (start us, length us, event | category | flops | bytes accessed | tf_op | source)
XLA Modules:
  0.0 1403.8 jit_solution(10777578352819962129)
XLA Ops:
  10.5 2.8 fusion.46
  13.5 9.4 fusion.3
  24.7 2.8 fusion.6
  27.5 7.1 fusion.113
  34.6 5.5 convert_bitcast_fusion
  40.1 5.2 copy.48
  45.3 5.8 reshape.333
  51.1 7.5 fusion.25
  58.7 16.3 %fusion.107 = f32[384,5632]{1,0:T(8,128)} fusion(bf16[2048,5632]{1,0:T(8,128)(2,1)} %param.26, bf16[384,2048]{1,0:T(8,128)(2,1)S(1)} %get-tuple-element.70, f32[2048]{0:T(1024)S(1)} %convert_element_type.162, f32[384]{0:T(512)S(1)} %add_rsqrt_fusion.1), kind=kOutput, calls=%fused_computation.169 | convolution fusion | flops 8861515776 | bytes 33302016 | tf_op jit(solution)/shard_map/dot_general | solution.py:553
  75.0 15.9 %fusion.109 = f32[384,5632]{1,0:T(8,128)} fusion(bf16[2048,5632]{1,0:T(8,128)(2,1)} %param.27, bf16[384,2048]{1,0:T(8,128)(2,1)S(1)} %get-tuple-element.70, f32[2048]{0:T(1024)S(1)} %convert_element_type.162, f32[384]{0:T(512)S(1)} %add_rsqrt_fusion.1), kind=kOutput, calls=%fused_computation.170 | convolution fusion | flops 8861515776 | bytes 33302016 | tf_op jit(solution)/shard_map/dot_general | solution.py:554
  91.0 27.0 %multiply_convert_fusion.1 = (bf16[384,5632]{1,0:T(8,128)(2,1)}, bf16[384,5632]{1,0:T(8,128)(2,1)}) fusion(f32[384,5632]{1,0:T(8,128)} %fusion.107, f32[384,5632]{1,0:T(8,128)} %fusion.109, bf16[384,2048]{1,0:T(8,128)(2,1)S(1)} %bitcast.328, bf16[5632,2048]{1,0:T(8,128)(2,1)} %param.28), kind=kOutput, calls=%fused_computation.6 | convolution fusion | flops 8886484992 | bytes 50593792 | tf_op jit(solution)/shard_map/nd,fd->nf/dot_general | solution.py:559
  118.0 16.4 %fusion.114 = f32[384,2048]{1,0:T(8,128)} fusion(bf16[384,5632]{1,0:T(8,128)(2,1)} %get-tuple-element.53, bf16[2048,5632]{1,0:T(8,128)(2,1)} %param.26), kind=kOutput, calls=%fused_computation.174 | convolution fusion | flops 8858370048 | bytes 30539776 | tf_op jit(solution)/shard_map/nf,df->nd/dot_general | solution.py:564
  134.3 17.2 %fusion.24 = (bf16[2048]{0:T(1024)(128)(2,1)S(1)}, f32[384]{0:T(512)S(1)}, f32[384,2048]{1,0:T(8,128)}) fusion(bf16[384,2048]{1,0:T(8,128)(2,1)} %copy-done.18, f32[384]{0:T(512)S(1)} %add_rsqrt_fusion.1, f32[2048]{0:T(1024)S(1)} %convert_element_type.162, f32[384,2048]{1,0:T(8,128)} %fusion.114, bf16[384,5632]{1,0:T(8,128)(2,1)} %get-tuple-element.52, ...), kind=kOutput, calls=%fused_computation.48 | convolution fusion | flops 8864659456 | bytes 35273728 | tf_op jit(solution)/shard_map/nf,df->nd/dot_general | solution.py:565
  151.6 3.4 fusion.23
  156.6 6.9 convolution_convert_fusion.5
  163.5 4.2 reshape.336
  167.7 5.4 copy.55
  173.2 4.9 fusion.59
  178.1 3.7 fusion.74
  181.7 13.3 fusion.44
  195.1 12.7 broadcast_multiply_fusion.1
  207.7 10.4 convolution_convert_fusion.3
  218.2 18.2 %convolution_convert_fusion.2 = bf16[2048,5632]{1,0:T(8,128)(2,1)} fusion(bf16[384,5632]{1,0:T(8,128)(2,1)} %get-tuple-element.53, bf16[384,2048]{1,0:T(8,128)(2,1)S(1)} %copy-done.19, f32[2048]{0:T(1024)S(1)} %convert_element_type.162, f32[384]{0:T(512)S(1)} %add_rsqrt_fusion.1), kind=kOutput, calls=%fused_computation.4 | convolution fusion | flops 8873050112 | bytes 28976640 | tf_op jit(solution)/shard_map/nd,nf->df/dot_general | solution.py:562
  236.4 19.2 %convolution_convert_fusion.1 = bf16[2048,5632]{1,0:T(8,128)(2,1)} fusion(bf16[384,5632]{1,0:T(8,128)(2,1)} %get-tuple-element.52, bf16[384,2048]{1,0:T(8,128)(2,1)} %copy-done.18, f32[2048]{0:T(1024)S(1)} %convert_element_type.162, f32[384]{0:T(512)S(1)} %add_rsqrt_fusion.1), kind=kOutput, calls=%fused_computation.3 | convolution fusion | flops 8873050112 | bytes 28976640 | tf_op jit(solution)/shard_map/nd,nf->df/dot_general | solution.py:563
  255.6 22.4 %convolution_convert_fusion = bf16[5632,2048]{1,0:T(8,128)(2,1)} fusion(bf16[384,2048]{1,0:T(8,128)(2,1)S(1)} %bitcast.329, f32[384,5632]{1,0:T(8,128)} %fusion.109, f32[384,5632]{1,0:T(8,128)} %fusion.107), kind=kOutput, calls=%fused_computation.2 | convolution fusion | flops 8882880512 | bytes 41943040 | tf_op jit(solution)/shard_map/nf,nd->fd/dot_general | solution.py:558
  278.6 3.9 broadcast_multiply_fusion
  285.0 4.9 fusion.7
  289.8 5.2 copy.52
  295.0 5.7 convert_element_type.171
  300.8 10.0 convolution_convert_fusion.4
  310.7 8.6 fusion.115
  322.3 3.5 fusion.116
  328.2 6.3 fusion.34
  334.5 3.4 copy-done.3
  337.8 55.6 %shard_map.272 = bf16[45056,8,128]{2,1,0:T(8,128)(2,1)} custom-call(bf16[2,8,128]{2,1,0:T(8,128)(2,1)S(1)} %bitcast.312, bf16[4096,8,128]{2,1,0:T(8,128)(2,1)S(1)} %bitcast.306, bf16[512,8,128]{2,1,0:T(8,128)(2,1)S(1)} %bitcast.308, bf16[512,8,128]{2,1,0:T(8,128)(2,1)S(1)} %bitcast.309, bf16[4096,8,128]{2,1,0:T(8,128)(2,1)S(1)} %bitcast.305, ...), custom_call_target="tpu_custom_call" | custom-call | flops 100000000 | bytes 176000000 | tf_op jit(solution)/shard_map/pallas_call | solution.py:473
  393.5 429.1 %shard_map.273 = (bf16[1408,8,128]{2,1,0:T(8,128)(2,1)}, bf16[32,704,8,128]{3,2,1,0:T(8,128)(2,1)}, bf16[16,704,8,128]{3,2,1,0:T(8,128)(2,1)}, bf16[8,704,8,128]...) custom-call(bf16[32,1408,8,128]{3,2,1,0:T(8,128)(2,1)} %bitcast.63.src_ref), custom_call_target="tpu_custom_call" | custom-call | tf_op jit(solution)/shard_map/pallas_call | solution.py:432
  832.4 46.0 %psum.7 = f32[]{:T(128)} all-reduce(f32[]{:T(128)} %multiply_reduce_fusion), channel_id=1, replica_groups=mesh['dp'=32] {'dp'}, use_global_device_ids=true, to_apply=%region_10.11 | all-reduce | flops 1 | bytes 8 | tf_op jit(solution)/shard_map/psum | solution.py:647
  879.2 15.2 %fusion.64 = (f32[1376384]{0:T(1024)}, f32[10753,128]{1,0:T(8,128)S(1)}, f32[1376384]{0:T(1024)}) fusion(f32[]{:T(128)S(6)} %mul.406, f32[11464,128]{1,0:T(8,128)} %copy-done.1, f32[1376384]{0:T(1024)} %param.31, f32[10753]{0:T(1024)S(1)} %fusion.90, f32[1376384]{0:T(1024)} %param.30, f32[1376384]{0:T(1024)} %param.29), kind=kLoop, calls=%fused_computation.98 | loop fusion | flops 22022144 | bytes 38581768 | tf_op jit(solution)/shard_map/reshape | solution.py:652
  898.4 3.8 shard_map.275.x_ref
  902.2 372.7 %shard_map.276 = bf16[32,1376,8,128]{3,2,1,0:T(8,128)(2,1)} custom-call(bf16[1376,8,128]{2,1,0:T(8,128)(2,1)S(1)} %shard_map.275.x_ref), custom_call_target="tpu_custom_call" | custom-call | tf_op jit(solution)/shard_map/pallas_call | solution.py:271
  1275.0 54.8 %shard_map.277 = (bf16[2,8,128]{2,1,0:T(8,128)(2,1)}, bf16[4096,8,128]{2,1,0:T(8,128)(2,1)S(1)}, bf16[512,8,128]{2,1,0:T(8,128)(2,1)S(1)}, bf16[512,8,128]{2,1,0...) custom-call(bf16[44032,8,128]{2,1,0:T(8,128)(2,1)} %bitcast.71.refs_0_), custom_call_target="tpu_custom_call" | custom-call | flops 100000000 | bytes 176000000 | tf_op jit(solution)/shard_map/pallas_call | solution.py:473
  1329.8 3.4 copy-done.4
  1333.2 9.8 copy.89
  1343.0 21.0 %reshape_reshape.12 = bf16[2048,32,64]{2,1,0:T(8,128)(2,1)} reshape(bf16[256,8,16,128]{3,2,1,0:T(8,128)(2,1)} %bitcast.314) | data formatting | bytes 16777216 | tf_op jit(solution)/shard_map/reshape;reshape | solution.py:617
  1364.0 18.3 %copy.61 = bf16[2048,32,64]{0,2,1:T(8,128)(2,1)} copy(bf16[2048,32,64]{2,1,0:T(8,128)(2,1)} %reshape_reshape.12) | data formatting | bytes 16777216
  1384.3 5.3 reshape_reshape.13
  1389.6 4.0 copy.62
  1395.7 4.4 reshape_reshape.14
  (115 shorter events, 41.8 us)
Async XLA Ops:
  0.6 7.9 copy-start
  0.7 7.5 copy-start.6
  3.6 893.4 %collective-permute-start = (f32[3,352,128]{2,1,0:T(8,128)}, f32[3,352,128]{2,1,0:T(8,128)}, u32[]{:S(2)}, u32[]{:S(2)}) collective-permute-start(f32[3,352,128]{2,1,0:T(8,128)} %pad_maximum_fusion), channel_id=1, source_target_pairs={{1,0},{2,1},{3,2},{4,3},{5,4},{6,5},{7,6},{8,7},{9,8},{10,9},{11,1... | collective-permute-start | bytes 1622024 | tf_op jit(solution)/shard_map/ppermute | solution.py:643
  5.6 2.9 copy-start.27
  8.5 1.1 copy-start.20
  10.5 2.9 copy-start.31
  10.5 2.9 copy-start.21
  24.4 3.1 copy-start.12
  24.4 3.1 copy-start.14
  24.6 2.8 copy-start.25
  51.1 7.6 copy-start.30
  58.7 16.4 %copy-start.18 = (bf16[384,2048]{1,0:T(8,128)(2,1)}, bf16[384,2048]{1,0:T(8,128)(2,1)S(1)}, u32[]{:S(2)}) copy-start(bf16[384,2048]{1,0:T(8,128)(2,1)S(1)} %get-tuple-element.70) | copy-start | bytes 4718596
  75.0 15.9 %copy-start.16 = (bf16[6,64,2048]{2,1,0:T(8,128)(2,1)S(1)}, bf16[6,64,2048]{2,1,0:T(8,128)(2,1)}, u32[]{:S(2)}) copy-start(bf16[6,64,2048]{2,1,0:T(8,128)(2,1)} %param.18) | copy-start | bytes 4718596
  154.9 1.7 copy-start.9
  173.2 4.9 copy-start.8
  178.0 3.7 copy-start.26
  181.7 13.3 copy-start.15
  207.7 10.5 copy-start.19
  236.4 19.2 %copy-start.17 = (bf16[6,64,2048]{2,1,0:T(8,128)(2,1)S(1)}, bf16[6,64,2048]{2,1,0:T(8,128)(2,1)}, u32[]{:S(2)}) copy-start(bf16[6,64,2048]{2,1,0:T(8,128)(2,1)} %param.18) | copy-start | bytes 4718596
  278.6 6.4 slice-start.2
  278.6 6.3 slice-start.3
  282.5 2.5 copy-start.13
  300.8 10.0 copy-start.22
  310.7 8.6 copy-start.24
  310.7 8.7 copy-start.23
  322.3 5.8 copy-start.28
  322.3 5.8 copy-start.29
  325.8 8.6 slice-start
  328.2 6.3 slice-start.1
  334.5 3.4 copy-start.3
  823.3 1.8 copy-start.5
  827.8 2.6 copy-start.1
  879.2 15.2 %copy-start.7 = (bf16[6,64,2048]{2,1,0:T(8,128)(2,1)S(1)}, bf16[6,64,2048]{2,1,0:T(8,128)(2,1)}, u32[]{:S(2)}) copy-start(bf16[6,64,2048]{2,1,0:T(8,128)(2,1)} %param.17) | copy-start | bytes 4718596
  879.2 15.2 %copy-start.10 = (f32[384,2048]{1,0:T(8,128)S(1)}, f32[384,2048]{1,0:T(8,128)}, u32[]{:S(2)}) copy-start(f32[384,2048]{1,0:T(8,128)} %copy-done.9) | copy-start | bytes 9437188
  879.2 15.2 %copy-start.11 = (f32[384,2048]{1,0:T(8,128)S(1)}, f32[384,2048]{1,0:T(8,128)}, u32[]{:S(2)}) copy-start(f32[384,2048]{1,0:T(8,128)} %get-tuple-element.74) | copy-start | bytes 9437188
  894.4 4.0 copy-start.2
  1329.8 3.4 copy-start.4

commit v2 on v1

v2 whole, which is shorter than its diff:
```python
import functools
import jax
import jax.numpy as jnp
import numpy as np
from jax import lax
from jax.experimental import pallas as pl
from jax.experimental.pallas import tpu as pltpu
from jax.sharding import PartitionSpec as P

NORM_EPS = 1e-5
ROPE_BASE = 10000.0
LEARN_RATE = 2e-3
BETA_ONE = 0.9
BETA_TWO = 0.95
ADAM_EPS = 1e-8
WEIGHT_DECAY = 0.1
STEP_COUNT = 100

MATS = ((2, 1), (4096, 16), (512, 2), (512, 2), (4096, 16), (2, 1), (11264, 44), (11264, 44), (11264, 16))
SUB, LANES = 8, 128
F32 = jnp.float32
OFFS = tuple(int(o) for o in np.cumsum([0] + [m[0] for m in MATS]))
NDEV = 32
TILES = OFFS[-1]
ROWS = TILES * 8 // NDEV
HALO = 352
WIN_R = 1408
WIN_A = 1376
S_ROWS = 11464
X_ROWS = 11112


def group_of(row):
    tile = row // 8
    mat = max(m for m in range(len(MATS)) if OFFS[m] <= tile)
    per = MATS[mat][1]
    return OFFS[mat] + (tile - OFFS[mat]) // per * per, per


def plan():
    lo, hi, own = [], [], []
    for dev in range(NDEV):
        start, per = group_of(ROWS * dev)
        last, last_per = group_of(ROWS * (dev + 1) - 1)
        lo.append(start)
        hi.append(last + last_per)
        own.append(start if start * SUB == ROWS * dev else start + per)
    own.append(TILES)
    return lo, hi, own


LO, HI, OWN = plan()
BASE = [min(a, TILES - WIN_R) for a in LO]


def overlap(a, b, mat):
    return max(a, OFFS[mat]), min(b, OFFS[mat + 1])


def tables():
    rows_in, rows_out = [], []
    for dev in range(NDEV):
        r_in, r_out = [], []
        for mat, (_, per) in enumerate(MATS):
            a, b = overlap(LO[dev], HI[dev], mat)
            n = max(0, b - a) // per
            r_in += [a - BASE[dev], SUB * a - ROWS * dev + HALO, n] if n else [0, 0, 0]
            a, b = overlap(OWN[dev], OWN[dev + 1], mat)
            n = max(0, b - a) // per
            r_out += [a - OWN[dev], SUB * a - ROWS * dev, n] if n else [0, 0, 0]
        rows_in.append(r_in)
        rows_out.append(r_out)
    return np.array(rows_in, np.int32), np.array(rows_out, np.int32)


def to_tiles(mat2d):
    rows, cols = mat2d.shape
    return mat2d.reshape(rows // SUB, SUB, cols // LANES, LANES).transpose(0, 2, 1, 3).reshape(-1, SUB, LANES)


def from_tiles(tiles, rows, cols):
    return tiles.reshape(rows // SUB, cols // LANES, SUB, LANES).transpose(0, 2, 1, 3).reshape(rows, cols)


def unpermute_kernel(tab, x_ref, o_ref):
    o_ref[0:HALO, :] = jnp.zeros((HALO, LANES), F32)
    o_ref[S_ROWS - HALO - 24:S_ROWS, :] = jnp.zeros((HALO + 24, LANES), F32)
    for mat, (_, per) in enumerate(MATS):
        t0, r0 = tab[3 * mat], tab[3 * mat + 1]

        def body(g, carry, per=per, t0=t0, r0=r0):
            for j in range(per):
                o_ref[pl.ds(r0 + g * (SUB * per) + j, SUB, stride=per), :] = x_ref[t0 + g * per + j].astype(F32)
            return carry

        lax.fori_loop(0, tab[3 * mat + 2], body, 0)


def unpermute(tab, win):
    return pl.pallas_call(
        unpermute_kernel,
        out_shape=jax.ShapeDtypeStruct((S_ROWS, LANES), F32),
        grid_spec=pltpu.PrefetchScalarGridSpec(
            num_scalar_prefetch=1, grid=(1,),
            in_specs=[pl.BlockSpec((WIN_R, SUB, LANES), lambda i, t: (0, 0, 0))],
            out_specs=pl.BlockSpec((S_ROWS, LANES), lambda i, t: (0, 0))),
        compiler_params=pltpu.CompilerParams(vmem_limit_bytes=40 << 20),
        cost_estimate=pl.CostEstimate(flops=4000000, bytes_accessed=9000000, transcendentals=0),
    )(tab, win)


def permute_kernel(tab, x_ref, h_ref, o_ref, s_ref):
    def fill(k, carry):
        at = pl.ds(pl.multiple_of(k * 64, 64), 64)
        s_ref[at, :] = x_ref[at, :]
        return carry

    lax.fori_loop(0, ROWS // 64, fill, 0)
    s_ref[ROWS // 64 * 64:ROWS, :] = x_ref[ROWS // 64 * 64:ROWS, :]
    s_ref[ROWS:ROWS + HALO, :] = h_ref[...]
    for mat, (_, per) in enumerate(MATS):
        t0, r0 = tab[3 * mat], tab[3 * mat + 1]

        def body(g, carry, per=per, t0=t0, r0=r0):
            for j in range(per):
                o_ref[t0 + g * per + j] = s_ref[pl.ds(r0 + g * (SUB * per) + j, SUB, stride=per), :].astype(jnp.bfloat16)
            return carry

        lax.fori_loop(0, tab[3 * mat + 2], body, 0)


def permute(tab, rows, halo):
    return pl.pallas_call(
        permute_kernel,
        out_shape=jax.ShapeDtypeStruct((WIN_A, SUB, LANES), jnp.bfloat16),
        grid_spec=pltpu.PrefetchScalarGridSpec(
            num_scalar_prefetch=1, grid=(1,),
            in_specs=[pl.BlockSpec((ROWS, LANES), lambda i, t: (0, 0)), pl.BlockSpec((HALO, LANES), lambda i, t: (0, 0))],
            out_specs=pl.BlockSpec((WIN_A, SUB, LANES), lambda i, t: (0, 0, 0)),
            scratch_shapes=[pltpu.VMEM((X_ROWS, LANES), F32)]),
        compiler_params=pltpu.CompilerParams(vmem_limit_bytes=40 << 20),
        cost_estimate=pl.CostEstimate(flops=4000000, bytes_accessed=9000000, transcendentals=0),
    )(tab, rows, halo)


SMALL = 152
ONE, TWO, SMALL_ONE, SMALL_TWO, SMALLS = range(5)


def parts_of(total):
    big = total // 2 - SMALL
    return (0, big), (big, big), (2 * big, SMALL), (2 * big + SMALL, SMALL), (2 * big, 2 * SMALL)


class Place:
    def __init__(self):
        me = lax.axis_index('dp')
        self.me = me
        self.core, self.xx, self.yy, self.zz = me % 2, (me // 2) % 2, (me // 4) % 2, me // 8
        self.mate, self.xn = self.at(self.zz, 0, 0, 1), self.at(self.zz, 0, 1, 0)
        self.yn, self.diag = self.at(self.zz, 1, 0, 0), self.at(self.zz, 1, 1, 0)
        self.up, self.down = self.at(self.zz + 1, 0, 0, 0), self.at(self.zz - 1, 0, 0, 0)
        self.has_up, self.has_down = self.zz < 3, self.zz > 0

    def at(self, z, dy, dx, dc):
        y, x, c = (1 - a if d else a for a, d in ((self.yy, dy), (self.xx, dx), (self.core, dc)))
        return ((z * 2 + y) * 2 + x) * 2 + c

    def greet(self):
        barrier = pltpu.get_barrier_semaphore()
        for cond, target in ((None, self.xn), (None, self.yn), (None, self.mate), (self.has_up, self.up), (self.has_down, self.down)):
            guarded(cond, lambda target=target: pl.semaphore_signal(
                barrier, device_id=(target,), device_id_type=pl.DeviceIdType.MESH))
        pl.semaphore_wait(barrier, 3 + self.has_up.astype(jnp.int32) + self.has_down.astype(jnp.int32))


def guarded(cond, body):
    if cond is None:
        body()
    else:
        pl.when(cond)(body)


def both(a, b):
    return b if a is None else a if b is None else jnp.logical_and(a, b)


def remote(src, dst, send, recv, target):
    return pltpu.make_async_remote_copy(src_ref=src, dst_ref=dst, send_sem=send, recv_sem=recv,
                                        device_id=(target,), device_id_type=pl.DeviceIdType.MESH)


PLANE = HERE, BY_X, BY_Y, BY_XY = (0, 0), (0, 1), (1, 0), (1, 1)


def gather_kernel(x_ref, out_ref, own_sem, send_sem, recv_sem):
    p = Place()
    p.greet()
    parts = parts_of(WIN_A)
    sent = []

    def view(slot, part, own=False):
        at = pl.ds(*parts[part])
        return x_ref.at[at] if own else out_ref.at[slot, at]

    def send(slot, part, target, cond=None, onward=None, own=False):
        desc = remote(view(slot, part, own), view(slot, part), send_sem.at[len(sent)], recv_sem.at[slot, part], target)
        sent.append((part, cond, onward))
        guarded(onward, desc.start)

    def arrived(slot, part):
        remote(view(slot, part), view(slot, part), send_sem.at[0], recv_sem.at[slot, part], p.mate).wait_recv()

    own_copy = pltpu.make_async_copy(x_ref, out_ref.at[p.me], own_sem)
    own_copy.start()
    send(p.me, SMALL_ONE, p.xn, own=True)
    send(p.me, SMALL_TWO, p.yn, own=True)
    for part in (ONE, TWO):
        send(p.me, part, p.up, None, p.has_up, True)
        send(p.me, part, p.down, None, p.has_down, True)
        send(p.me, part, p.xn, own=True)
        send(p.me, part, p.yn, own=True)
    send(p.me, SMALL_ONE, p.yn, own=True)
    send(p.me, SMALL_TWO, p.xn, own=True)
    for part in (ONE, TWO, SMALLS):
        send(p.me, part, p.mate, own=True)
    arrived(p.xn, SMALL_ONE)
    send(p.xn, SMALL_ONE, p.yn)
    arrived(p.yn, SMALL_TWO)
    send(p.yn, SMALL_TWO, p.xn)

    def steps(step):
        if step == 0:
            return [(None, p.zz, None, None)]
        return [(p.zz >= step, p.zz - step, p.up, p.has_up), (p.zz + step <= 3, p.zz + step, p.down, p.has_down)]

    def column(step):
        for cond, z, to, onward in steps(step):
            def body():
                slot = p.at(z, *HERE, 0)
                for part in (ONE, TWO):
                    arrived(slot, part)
                    send(slot, part, to, cond, onward)
                    for target in (p.xn, p.yn, p.mate):
                        send(slot, part, target, cond)
            guarded(cond, body)

    def beside(step):
        for cond, z, _, _ in steps(step):
            def body():
                for part in (ONE, TWO):
                    for dy, dx in (BY_X, BY_Y):
                        slot = p.at(z, dy, dx, 0)
                        arrived(slot, part)
                        if dy == part:
                            send(slot, part, p.xn if dy else p.yn, cond)
                        send(slot, part, p.mate, cond)
            guarded(cond, body)

    def across(step):
        for cond, z, _, _ in steps(step):
            def body():
                slot = p.at(z, *BY_XY, 0)
                for part in (ONE, TWO):
                    arrived(slot, part)
                    send(slot, part, p.mate, cond)
            guarded(cond, body)

    def plane():
        for dy, dx in PLANE:
            slot = p.at(p.zz, dy, dx, 0)
            own = dy + dx == 0
            if not own:
                if dy:
                    arrived(slot, SMALL_ONE)
                if dx:
                    arrived(slot, SMALL_TWO)
                send(slot, SMALLS, p.mate)
            send(slot, SMALLS, p.up, None, p.has_up, own)
            send(slot, SMALLS, p.down, None, p.has_down, own)

    def planes(step):
        for cond, z, to, onward in steps(step):
            def body():
                for dy, dx in PLANE:
                    slot = p.at(z, dy, dx, 0)
                    arrived(slot, SMALLS)
                    send(slot, SMALLS, to, cond, onward)
                    send(slot, SMALLS, p.mate, cond)
            guarded(cond, body)

    column(1)
    beside(0)
    column(2)
    plane()
    beside(1)
    across(0)
    column(3)
    beside(2)
    across(1)
    planes(1)
    beside(3)
    across(2)
    planes(2)
    across(3)
    planes(3)

    def drain(k, carry):
        for part in (ONE, TWO, SMALLS):
            arrived(2 * k + 1 - p.core, part)
        return carry

    lax.fori_loop(0, NDEV // 2, drain, 0)
    for k, (part, cond, onward) in enumerate(sent):
        done = remote(view(p.me, part), view(p.me, part), send_sem.at[k], recv_sem.at[p.me, part], p.mate).wait_send
        guarded(both(cond, onward), done)
    own_copy.wait()


def gather(shard):
    dma = pltpu.SemaphoreType.DMA
    return pl.pallas_call(
        gather_kernel,
        out_shape=jax.ShapeDtypeStruct((NDEV, WIN_A, SUB, LANES), jnp.bfloat16),
        in_specs=[pl.BlockSpec(memory_space=pltpu.VMEM)],
        out_specs=pl.BlockSpec(memory_space=pl.ANY),
        scratch_shapes=[dma, dma((200,)), dma((NDEV, 5))],
        compiler_params=pltpu.CompilerParams(collective_id=1, has_side_effects=True, vmem_limit_bytes=16 << 20),
    )(shard)


PIECES = ((*BY_XY, ONE), (*BY_XY, TWO), (*BY_Y, ONE), (*BY_X, TWO), (*BY_X, ONE), (*BY_Y, TWO), (*HERE, ONE), (*HERE, TWO))


def scatter_kernel(src_ref, out_ref, land_mate, land_hop, land_z, acc, tmp, load_sem, tmp_sem, out_sem, send_sem, mate_sem, hop_sem, z_sem):
    p = Place()
    p.greet()
    parts = parts_of(WIN_R)
    sent = []

    low = jnp.minimum(p.zz, 3 - p.zz)
    order = []
    for far, near in ((3, 3), (2, 0), (1, 2)):
        at = jnp.where(low == 0, far, near)
        order.append(jnp.where(p.zz >= 2, 3 - at, at))
    order.append(p.zz)

    def here(k, dy, dx, part):
        return acc.at[k * 4 + dy * 2 + dx, pl.ds(*parts[part])]

    def fetch(k, dy, dx, part):
        at, i = pl.ds(*parts[part]), k * 4 + dy * 2 + dx
        own = pltpu.make_async_copy(src_ref.at[p.at(order[k], dy, dx, 0), at], here(k, dy, dx, part), load_sem.at[i, min(part, 2)])
        give = remote(src_ref.at[p.at(order[k], dy, dx, 1), at], land_mate.at[i, at], send_sem.at[i, min(part, 2)], mate_sem.at[i, min(part, 2)], p.mate)
        return own, give, land_mate.at[i, at]

    def add(k, dy, dx, part, landed):
        start, count = parts[part]
        copy = pltpu.make_async_copy(landed, tmp.at[pl.ds(0, count)], tmp_sem)
        copy.start()
        copy.wait()
        i = k * 4 + dy * 2 + dx

        def body(t, carry):
            at, to = pl.ds(t * SUB, SUB), pl.ds(start + t * SUB, SUB)
            acc[i, to] = (acc[i, to].astype(F32) + tmp[at].astype(F32)).astype(jnp.bfloat16)
            return carry

        lax.fori_loop(0, count // SUB, body, 0)

    def begin(k, pieces):
        for piece in pieces:
            own, give, _ = fetch(k, *piece)
            give.start()
            own.start()

    def join(k, piece):
        own, give, landed = fetch(k, *piece)
        own.wait()
        give.wait_recv()
        add(k, *piece, landed)

    def hop(k, dy, dx, part, second):
        by_y = (part in (ONE, SMALL_ONE)) != second
        to_dy, to_dx = (0, dx) if by_y else (dy, 0)
        n = to_dy + to_dx + 2 * second
        dst = land_hop.at[k, n, pl.ds(*parts[part])]
        desc = remote(here(k, dy, dx, part), dst, send_sem.at[16 + k * 3 + n, part], hop_sem.at[k, n, part], p.yn if by_y else p.xn)
        return desc, dst, (16 + k * 3 + n, part)

    def leave(k, dy, dx, part, second=False):
        desc, _, key = hop(k, dy, dx, part, second)
        sent.append((key, part))
        desc.start()

    def enter(k, dy, dx, part, second=False):
        by_y = (part in (ONE, SMALL_ONE)) != second
        frm = (1, dx) if by_y else (dy, 1)
        desc, landed, _ = hop(k, *frm, part, second)
        desc.wait_recv()
        add(k, dy, dx, part, landed)

    def along(k, dy, dx, part, way):
        n = dy * 2 + dx
        at = pl.ds(*parts[part])
        key = (28 + k * 4 + n, min(part, 2))
        return remote(here(k, dy, dx, part), land_z.at[way, order[k], n, at], send_sem.at[key], z_sem.at[way, order[k], n, min(part, 2)],
                      p.down if way else p.up), land_z.at[way, order[k], n, at], key

    def collect(k, dy, dx, part):
        for way, cond in ((0, (order[k] >= p.zz) & p.has_down), (1, (order[k] <= p.zz) & p.has_up)):
            @pl.when(cond)
            def _():
                desc, landed, _ = along(k, dy, dx, part, way)
                desc.wait_recv()
                add(k, dy, dx, part, landed)

    def pass_on(k, dy, dx, part):
        for way, cond in ((0, order[k] > p.zz), (1, order[k] < p.zz)):
            @pl.when(cond)
            def _():
                along(k, dy, dx, part, way)[0].start()

    smalls = [(dy, dx, SMALLS) for dy, dx in PLANE]
    begin(0, smalls)
    begin(0, PIECES)
    begin(1, smalls)
    begin(2, smalls)
    begin(1, PIECES)
    begin(2, PIECES)
    begin(3, smalls)
    begin(3, PIECES)

    is_end = low == 0

    def small(k):
        for piece in smalls:
            join(k, piece)
        if k < 3:
            for piece in smalls:
                sent.append((along(k, *piece, 0)[2], SMALLS))
            pl.when(is_end)(lambda: [pass_on(k, *piece) for piece in smalls] and None)

    def chain(k):
        @pl.when(jnp.logical_not(is_end))
        def _():
            for piece in smalls:
                collect(k, *piece)
                pass_on(k, *piece)

    def prepare(k):
        for piece in PIECES:
            join(k, piece)
            if piece[piece[2]] == 1:
                leave(k, *piece)

    def second(k):
        for piece in ((*BY_X, ONE), (*BY_Y, TWO)):
            enter(k, *piece)
            leave(k, *piece, True)

    def final(k):
        for part in (ONE, TWO):
            enter(k, *HERE, part)
        for part in (ONE, TWO):
            enter(k, *HERE, part, True)
            collect(k, *HERE, part)
            if k < 3:
                sent.append((along(k, *HERE, part, 0)[2], part))
                pass_on(k, *HERE, part)

    small(0)
    prepare(0)
    small(1)
    small(2)
    prepare(1)
    chain(0)
    small(3)
    second(0)
    prepare(2)
    chain(1)
    second(1)
    chain(2)
    prepare(3)
    for piece in smalls:
        collect(3, *piece)
    for dy, dx, part in ((*BY_XY, SMALL_ONE), (*BY_XY, SMALL_TWO), (*BY_Y, SMALL_ONE), (*BY_X, SMALL_TWO)):
        leave(3, dy, dx, part)
    final(0)
    for piece in ((*BY_X, SMALL_ONE), (*BY_Y, SMALL_TWO)):
        enter(3, *piece)
        leave(3, *piece, True)
    second(2)
    final(1)
    second(3)
    for part in (SMALL_ONE, SMALL_TWO):
        enter(3, *HERE, part)
        enter(3, *HERE, part, True)
    final(2)
    final(3)
    out = pltpu.make_async_copy(acc.at[12], out_ref, out_sem)
    out.start()
    for k in range(4):
        for piece in PIECES + tuple(smalls):
            fetch(k, *piece)[1].wait_send()
    for key, part in sent:
        src = here(0, *HERE, part)
        remote(src, src, send_sem.at[key], z_sem.at[0, 0, 0, 0], p.mate).wait_send()
    out.wait()


def scatter(slots):
    def lands(*lead):
        return jax.ShapeDtypeStruct(lead + (WIN_R, SUB, LANES), jnp.bfloat16)

    any_spec = pl.BlockSpec(memory_space=pl.ANY)
    dma = pltpu.SemaphoreType.DMA
    return pl.pallas_call(
        scatter_kernel,
        out_shape=(lands(), lands(16), lands(4, 3), lands(2, 4, 4)),
        in_specs=[any_spec],
        out_specs=(any_spec,) * 4,
        scratch_shapes=[pltpu.VMEM((16, WIN_R, SUB, LANES), jnp.bfloat16), pltpu.VMEM((WIN_R // 2, SUB, LANES), jnp.bfloat16),
                        dma((16, 3)), dma, dma, dma((44, 4)), dma((16, 3)), dma((4, 3, 4)), dma((2, 4, 4, 3))],
        compiler_params=pltpu.CompilerParams(collective_id=2, has_side_effects=True, vmem_limit_bytes=56 << 20),
    )(slots)[0]


BUFS = 6


def move_kernel(moves, n_in, n_out, *refs):
    ins, outs = refs[:n_in], refs[n_in:n_in + n_out]
    buf, in_sem, out_sem = refs[n_in + n_out:]

    def read(n):
        src, a, _, _, count = moves[n]
        return pltpu.make_async_copy(ins[src].at[pl.ds(a, count)], buf.at[n % BUFS, pl.ds(0, count)], in_sem.at[n % BUFS])

    def write(n):
        _, _, dst, b, count = moves[n]
        return pltpu.make_async_copy(buf.at[n % BUFS, pl.ds(0, count)], outs[dst].at[pl.ds(b, count)], out_sem.at[n % BUFS])

    ahead = BUFS // 2
    for n in range(len(moves) + ahead):
        if n < len(moves):
            if n >= BUFS:
                write(n - BUFS).wait()
            read(n).start()
        if n >= ahead:
            read(n - ahead).wait()
            write(n - ahead).start()
    for n in range(max(0, len(moves) - BUFS), len(moves)):
        write(n).wait()


def move(moves, arrays, out_tiles):
    moves = tuple(m[:1] + (m[1] + c,) + m[2:3] + (m[3] + c, min(BLOCK, m[4] - c)) for m in moves for c in range(0, m[4], BLOCK))
    return pl.pallas_call(
        functools.partial(move_kernel, moves, len(arrays), len(out_tiles)),
        out_shape=tuple(jax.ShapeDtypeStruct((n, SUB, LANES), jnp.bfloat16) for n in out_tiles),
        in_specs=[pl.BlockSpec(memory_space=pl.ANY)] * len(arrays),
        out_specs=(pl.BlockSpec(memory_space=pl.ANY),) * len(out_tiles),
        scratch_shapes=[pltpu.VMEM((BUFS, BLOCK, SUB, LANES), jnp.bfloat16), pltpu.SemaphoreType.DMA((BUFS,)),
                        pltpu.SemaphoreType.DMA((BUFS,))],
        compiler_params=pltpu.CompilerParams(vmem_limit_bytes=20 << 20),
        cost_estimate=pl.CostEstimate(flops=100000000, bytes_accessed=176000000, transcendentals=0),
    )(*arrays)


BLOCK = 704


def norm_kernel(part_ref, out_ref, held, land, send_sem, recv_sem):
    me = lax.axis_index('dp')
    peers = [me + bit * (1 - 2 * ((me // bit) % 2)) for bit in (1, 2, 4, 8, 16)]
    barrier = pltpu.get_barrier_semaphore()
    for peer in peers:
        pl.semaphore_signal(barrier, inc=1, device_id=(peer,), device_id_type=pl.DeviceIdType.MESH)
    pl.semaphore_wait(barrier, 5)
    held[0] = part_ref[...]
    for n, peer in enumerate(peers):
        copy = pltpu.make_async_remote_copy(
            src_ref=held.at[n], dst_ref=land.at[n], send_sem=send_sem.at[n], recv_sem=recv_sem.at[n],
            device_id=(peer,), device_id_type=pl.DeviceIdType.MESH)
        copy.start()
        copy.wait()
        if n < 4:
            held[n + 1] = held[n] + land[n]
        else:
            out_ref[...] = held[n] + land[n]


def sum_over_devices(part):
    vmem = pl.BlockSpec(memory_space=pltpu.VMEM)
    rounds = pltpu.VMEM((5, SUB, LANES), F32)
    total = pl.pallas_call(
        norm_kernel,
        out_shape=jax.ShapeDtypeStruct((SUB, LANES), F32),
        in_specs=[vmem], out_specs=vmem,
        scratch_shapes=[rounds, rounds] + [pltpu.SemaphoreType.DMA((5,))] * 2,
        compiler_params=pltpu.CompilerParams(collective_id=3, has_side_effects=True, vmem_limit_bytes=4 << 20),
    )(jnp.full((SUB, LANES), part, F32))
    return total[0, 0]


def turn_kernel(x_ref, o_ref):
    rows = x_ref.shape[0] * 8
    o_ref[...] = x_ref[...].astype(F32).reshape(rows, LANES).T.astype(jnp.bfloat16)


def turned(tiles, rows, cols):
    return pl.pallas_call(
        turn_kernel,
        out_shape=jax.ShapeDtypeStruct((cols, rows), jnp.bfloat16),
        grid=(cols // LANES, rows // 1024),
        in_specs=[pl.BlockSpec((LANES, None, SUB, LANES), lambda j, i: (i, j, 0, 0))],
        out_specs=pl.BlockSpec((LANES, 1024), lambda j, i: (j, i)),
        cost_estimate=pl.CostEstimate(flops=rows * cols, bytes_accessed=4 * rows * cols, transcendentals=0),
    )(tiles.reshape(rows // SUB, cols // LANES, SUB, LANES))


def rope_tables(positions, head_dim):
    half_dim = head_dim // 2
    inv_freq = ROPE_BASE ** (-2.0 * jnp.arange(half_dim, dtype=F32) / head_dim)
    angles = positions.astype(F32)[:, :, None] * inv_freq
    cos_full = jnp.concatenate([jnp.cos(angles), jnp.cos(angles)], axis=-1)[:, :, None, :]
    sin_full = jnp.concatenate([jnp.sin(angles), jnp.sin(angles)], axis=-1)[:, :, None, :]
    return cos_full, sin_full


def rope_apply(values, cos_full, sin_full):
    half_dim = values.shape[-1] // 2
    rotated = jnp.concatenate([-values[..., half_dim:], values[..., :half_dim]], axis=-1)
    return values * cos_full + rotated * sin_full


def rope_back(grad_rot, cos_full, sin_full):
    half_dim = grad_rot.shape[-1] // 2
    scaled = grad_rot * sin_full
    return grad_rot * cos_full + jnp.concatenate([scaled[..., half_dim:], -scaled[..., :half_dim]], axis=-1)


def rms_parts(values):
    inv_rms = lax.rsqrt(jnp.mean(values * values, axis=-1, keepdims=True) + NORM_EPS)
    return inv_rms, values * inv_rms


def rms_back(d_normed, gain_wide, inv_rms, x_hat):
    d_hat = d_normed * gain_wide
    return inv_rms * (d_hat - x_hat * jnp.mean(d_hat * x_hat, axis=-1, keepdims=True))


def local_grads(x_loc, dy_loc, pos_loc, w_list):
    attn_gain, w_query, w_key, w_value, w_out, mlp_gain, w_gate, w_up, w_down = w_list
    num_seqs, seq_len, model_dim = x_loc.shape
    num_heads, head_dim = w_query.shape[1], w_query.shape[2]
    kv_heads = w_key.shape[1]
    group_size = num_heads // kv_heads
    n_tok = num_seqs * seq_len
    wq_flat = w_query.reshape(model_dim, num_heads * head_dim)
    wk_flat = w_key.reshape(model_dim, kv_heads * head_dim)
    wv_flat = w_value.reshape(model_dim, kv_heads * head_dim)
    wo_flat = w_out.reshape(num_heads * head_dim, model_dim)
    dy_flat = dy_loc.reshape(n_tok, model_dim)
    x_wide = x_loc.reshape(n_tok, model_dim).astype(F32)
    inv_one, value_a8 = rms_parts(x_wide)
    gain_one = attn_gain.astype(F32)
    normed = (value_a8 * gain_one).astype(jnp.bfloat16)
    q_pre = jnp.dot(normed, wq_flat, preferred_element_type=F32).reshape(num_seqs, seq_len, num_heads, head_dim)
    k_pre = jnp.dot(normed, wk_flat, preferred_element_type=F32).reshape(num_seqs, seq_len, kv_heads, head_dim)
    v_heads = jnp.dot(normed, wv_flat, preferred_element_type=F32).astype(jnp.bfloat16).reshape(num_seqs, seq_len, kv_heads, head_dim)
    cos_full, sin_full = rope_tables(pos_loc, head_dim)
    q_rot = rope_apply(q_pre, cos_full, sin_full).astype(jnp.bfloat16).reshape(num_seqs, seq_len, kv_heads, group_size, head_dim)
    k_rot = rope_apply(k_pre, cos_full, sin_full).astype(jnp.bfloat16)
    score_scale = head_dim ** -0.5
    scores = jnp.einsum('bqkgd,bskd->bkgqs', q_rot, k_rot, preferred_element_type=F32) * score_scale
    causal = lax.iota(jnp.int32, seq_len)[:, None] >= lax.iota(jnp.int32, seq_len)[None, :]
    attn_probs = jax.nn.softmax(jnp.where(causal, scores, -1e30), axis=-1)
    probs_low = attn_probs.astype(jnp.bfloat16)
    context = jnp.einsum('bkgqs,bskd->bqkgd', probs_low, v_heads, preferred_element_type=F32).astype(jnp.bfloat16)
    context = context.reshape(n_tok, num_heads * head_dim)
    attn_out = jnp.dot(context, wo_flat, preferred_element_type=F32)
    hidden = (x_wide + attn_out).astype(jnp.bfloat16)
    inv_two, array_b8 = rms_parts(hidden.astype(F32))
    gain_two = mlp_gain.astype(F32)
    normed_mlp = (array_b8 * gain_two).astype(jnp.bfloat16)
    gate_pre = jnp.dot(normed_mlp, w_gate, preferred_element_type=F32)
    up_pre = jnp.dot(normed_mlp, w_up, preferred_element_type=F32)
    gate_sig = jax.nn.sigmoid(gate_pre)
    gate_act = gate_pre * gate_sig
    gated_act = (gate_act * up_pre).astype(jnp.bfloat16)
    g_down = jnp.einsum('nf,nd->fd', gated_act, dy_flat, preferred_element_type=F32)
    d_gated = jnp.einsum('nd,fd->nf', dy_flat, w_down, preferred_element_type=F32)
    d_up = (d_gated * gate_act).astype(jnp.bfloat16)
    d_gate = (d_gated * up_pre * gate_sig * (1.0 + gate_pre * (1.0 - gate_sig))).astype(jnp.bfloat16)
    g_gate = jnp.einsum('nd,nf->df', normed_mlp, d_gate, preferred_element_type=F32)
    g_up = jnp.einsum('nd,nf->df', normed_mlp, d_up, preferred_element_type=F32)
    d_normed_mlp = (jnp.einsum('nf,df->nd', d_gate, w_gate, preferred_element_type=F32)
                    + jnp.einsum('nf,df->nd', d_up, w_up, preferred_element_type=F32))
    g_mlp_gain = jnp.sum(d_normed_mlp * array_b8, axis=0)
    d_hidden = rms_back(d_normed_mlp, gain_two, inv_two, array_b8) + dy_flat.astype(F32)
    d_hidden_low = d_hidden.astype(jnp.bfloat16)
    g_out = jnp.einsum('nc,nd->cd', context, d_hidden_low, preferred_element_type=F32)
    d_context = jnp.einsum('nd,cd->nc', d_hidden_low, wo_flat, preferred_element_type=F32).astype(jnp.bfloat16)
    d_context = d_context.reshape(num_seqs, seq_len, kv_heads, group_size, head_dim)
    d_probs = jnp.einsum('bqkgd,bskd->bkgqs', d_context, v_heads, preferred_element_type=F32)
    g_values = jnp.einsum('bkgqs,bqkgd->bskd', probs_low, d_context, preferred_element_type=F32)
    d_scores = (attn_probs * (d_probs - jnp.sum(d_probs * attn_probs, axis=-1, keepdims=True)) * score_scale).astype(jnp.bfloat16)
    d_q_rot = jnp.einsum('bkgqs,bskd->bqkgd', d_scores, k_rot, preferred_element_type=F32).reshape(num_seqs, seq_len, num_heads, head_dim)
    d_k_rot = jnp.einsum('bkgqs,bqkgd->bskd', d_scores, q_rot, preferred_element_type=F32)
    d_q_pre = rope_back(d_q_rot, cos_full, sin_full).astype(jnp.bfloat16).reshape(n_tok, num_heads * head_dim)
    d_k_pre = rope_back(d_k_rot, cos_full, sin_full).astype(jnp.bfloat16).reshape(n_tok, kv_heads * head_dim)
    d_v_pre = g_values.astype(jnp.bfloat16).reshape(n_tok, kv_heads * head_dim)
    g_query = jnp.einsum('nd,nc->dc', normed, d_q_pre, preferred_element_type=F32)
    g_key = jnp.einsum('nd,nc->dc', normed, d_k_pre, preferred_element_type=F32)
    g_value = jnp.einsum('nd,nc->dc', normed, d_v_pre, preferred_element_type=F32)
    d_normed = (jnp.einsum('nc,dc->nd', d_q_pre, wq_flat, preferred_element_type=F32)
                + jnp.einsum('nc,dc->nd', d_k_pre, wk_flat, preferred_element_type=F32)
                + jnp.einsum('nc,dc->nd', d_v_pre, wv_flat, preferred_element_type=F32))
    g_attn_gain = jnp.sum(d_normed * value_a8, axis=0)
    d_x = rms_back(d_normed, gain_one, inv_one, value_a8) + d_hidden
    grad_list = [g_attn_gain, g_query, g_key, g_value, g_out, g_mlp_gain, g_gate, g_up, g_down]
    return d_x.astype(jnp.bfloat16).reshape(num_seqs, seq_len, model_dim), grad_list


def windows(grad_list):
    tiles = [g.astype(jnp.bfloat16).reshape(2, SUB, LANES) if g.ndim == 1 else to_tiles(g.astype(jnp.bfloat16)) for g in grad_list]
    moves = []
    for dev in range(NDEV):
        for mat in range(len(MATS)):
            a, b = overlap(BASE[dev], BASE[dev] + WIN_R, mat)
            if b > a:
                moves.append((mat, a - OFFS[mat], 0, dev * WIN_R + a - BASE[dev], b - a))
    return move(moves, tiles, (NDEV * WIN_R,))[0].reshape(NDEV, WIN_R, SUB, LANES)


def assemble(slots, w_list):
    moves = []
    for dev in range(NDEV):
        for mat in range(len(MATS)):
            a, b = overlap(OWN[dev], OWN[dev + 1], mat)
            if b > a:
                moves.append((0, dev * WIN_A + a - OWN[dev], mat, a - OFFS[mat], b - a))
    tiles = move(moves, [slots.reshape(NDEV * WIN_A, SUB, LANES)], tuple(m[0] for m in MATS))
    out = []
    for mat, weight in enumerate(w_list):
        if weight.ndim == 1:
            out.append(tiles[mat].reshape(weight.shape))
        else:
            cols = MATS[mat][1] * LANES
            rows = weight.size // cols
            if mat in (1, 2, 3):
                flat = turned(tiles[mat], rows, cols)
                out.append(flat.reshape(weight.shape[1:] + weight.shape[:1]).transpose(2, 0, 1))
            else:
                out.append(from_tiles(tiles[mat], rows, cols).reshape(weight.shape))
    return out


def reduce_scatter(grad_list):
    return scatter(windows(grad_list))


def adamw(grad, clip_scale, master, mean, var, first_row):
    clipped = grad * clip_scale
    new_mean = BETA_ONE * mean + (1.0 - BETA_ONE) * clipped
    new_var = BETA_TWO * var + (1.0 - BETA_TWO) * clipped * clipped
    mean_hat = new_mean / (1.0 - BETA_ONE ** STEP_COUNT)
    var_hat = new_var / (1.0 - BETA_TWO ** STEP_COUNT)
    row = first_row + lax.broadcasted_iota(jnp.int32, master.shape, 0)
    gain_two = OFFS[5] * 8
    is_gain = (row < 16) | ((row >= gain_two) & (row < gain_two + 16))
    decays = jnp.where(is_gain, 0.0, WEIGHT_DECAY)
    new_master = master - LEARN_RATE * (mean_hat / (jnp.sqrt(var_hat) + ADAM_EPS) + decays * master)
    return new_master, new_mean, new_var


def update(win, master, mean, var, tab_in, tab_out):
    me = lax.axis_index('dp')
    state = [s.reshape(ROWS, LANES) for s in (master, mean, var)]
    edge = jnp.stack([s[:HALO] for s in state])
    edge = lax.ppermute(edge, 'dp', [(d, d - 1) for d in range(1, NDEV)])
    summed = unpermute(jnp.asarray(tab_in)[me], win)
    grad = summed[HALO:HALO + ROWS] * (1.0 / NDEV)
    grad_edge = summed[HALO + ROWS:2 * HALO + ROWS] * (1.0 / NDEV)
    grad_norm = jnp.sqrt(sum_over_devices(jnp.sum(grad * grad)))
    clip_scale = jnp.minimum(1.0, 1.0 / (grad_norm + 1e-6))
    new_state = adamw(grad, clip_scale, *state, me * ROWS)
    edge_master = adamw(grad_edge, clip_scale, edge[0], edge[1], edge[2], (me + 1) * ROWS)[0]
    shard = permute(jnp.asarray(tab_out)[me], new_state[0], edge_master)
    return [s.reshape(-1) for s in new_state], grad_norm, shard


def solution(mesh):
    tab_in, tab_out = tables()

    def per_device(x_loc, dy_loc, pos_loc, attn_gain, w_query, w_key, w_value, w_out, mlp_gain, w_gate, w_up, w_down, master_loc, mean_loc, var_loc):
        w_list = (attn_gain, w_query, w_key, w_value, w_out, mlp_gain, w_gate, w_up, w_down)
        grad_x, grad_list = local_grads(x_loc, dy_loc, pos_loc, w_list)
        win = reduce_scatter(grad_list)
        new_state, grad_norm, shard = update(win, master_loc, mean_loc, var_loc, tab_in, tab_out)
        new_weights = assemble(gather(shard), w_list)
        return (grad_x,) + tuple(new_weights) + tuple(new_state) + (grad_norm,)

    in_specs = (P('dp'),) * 3 + (P(),) * 9 + (P('dp'),) * 3
    out_specs = (P('dp'),) + (P(),) * 9 + (P('dp'),) * 3 + (P(),)
    return jax.shard_map(per_device, mesh=mesh, in_specs=in_specs, out_specs=out_specs, check_vma=False)
```

time: 1410 us -> 1330 us (0.943)
  local copies, waits for them, and re-layouts: 120 us -> 59.5 us
  blocking collectives: 46 us -> 0 us
  Pallas kernels: 919 us -> 945 us
    psum x1 -> x0, blocking collectives: 46 us -> none  [update(): grad_norm = jnp.sqrt(lax.psum(jnp.sum(grad * grad), 'dp'))]
    another operation x3 -> x0, local copies, waits for them, and re-layouts: 30.7 us -> none  [assemble(): from_tiles(tiles[mat], weight.size // cols, cols).reshape(weight.shape)]
    pallas_call x1, Pallas kernels: 373 us -> 392 us  [gather(): pl.pallas_call(gather_kernel, out_shape=jax.ShapeDtypeStruct((NDEV, WIN_A...]
    unnamed x75 -> x84, local copies, waits for them, and re-layouts: 38.8 us -> 20.3 us
    pallas_call x2 -> x6, Pallas kernels: 433 us -> 440 us  [the longest x1 389 us: scatter(): pl.pallas_call(scatter_kernel, out_shape=(lands(), lands(16), lands(4, 3)...]
  transfers between devices with their start and end apart: 1 -> 1, of which waited for: 0 -> 0; matrix products, arithmetic and copies ran while one was open for 25% -> 26% of each run, Pallas kernels for 35% -> 35%
where the time goes in v2:
time: 1330 us; the launch traced here: 1320 us
  Pallas kernels  945 us (71%)
  matrix products  265 us (20%)
  local copies, waits for them, and re-layouts  59.5 us (4%)
  other arithmetic  47.2 us (4%)
    pallas_call x1, Pallas kernels, gather(): pl.pallas_call(gather_kernel, out_shape=jax.ShapeDtypeStruct((NDEV, WIN_A...  392 us
    pallas_call x1, Pallas kernels, scatter(): pl.pallas_call(scatter_kernel, out_shape=(lands(), lands(16), lands(4, 3)...  389 us
    pallas_call x2, Pallas kernels, move(): pl.pallas_call(functools.partial(move_kernel, moves, len(arrays), len(out...  110 us
    pallas_call x3, Pallas kernels, turned(): pl.pallas_call(turn_kernel, out_shape=jax.ShapeDtypeStruct((cols, rows),...  27.8 us
    dot_general x1, matrix products, local_grads(): jnp.einsum('nd,fd->nf', dy_flat, w_down, preferred_element_type=F32)  27 us
  transfers between devices with their start and end apart: 1, of which 0 were waited for; matrix products, arithmetic and copies ran while one was open for 26% of the time, Pallas kernels for 35%

profile of v2, /device:TPU:0, one launch (start us, length us, event | category | flops | bytes accessed | tf_op | source)
XLA Modules:
  0.0 1320.9 jit_solution(4868720658702637486)
XLA Ops:
  10.6 2.8 fusion.46
  13.5 9.5 fusion.3
  24.8 2.8 fusion.6
  27.6 7.1 fusion.113
  34.7 5.5 convert_bitcast_fusion
  40.2 5.2 copy.45
  45.4 6.1 reshape.343
  51.6 7.5 fusion.25
  59.0 16.4 %fusion.107 = f32[384,5632]{1,0:T(8,128)} fusion(bf16[2048,5632]{1,0:T(8,128)(2,1)} %param.26, bf16[384,2048]{1,0:T(8,128)(2,1)S(1)} %get-tuple-element.56, f32[2048]{0:T(1024)S(1)} %convert_element_type.162, f32[384]{0:T(512)S(1)} %add_rsqrt_fusion.1), kind=kOutput, calls=%fused_computation.166 | convolution fusion | flops 8861515776 | bytes 33302016 | tf_op jit(solution)/shard_map/dot_general | solution.py:688
  75.5 15.9 %fusion.109 = f32[384,5632]{1,0:T(8,128)} fusion(bf16[2048,5632]{1,0:T(8,128)(2,1)} %param.27, bf16[384,2048]{1,0:T(8,128)(2,1)S(1)} %get-tuple-element.56, f32[2048]{0:T(1024)S(1)} %convert_element_type.162, f32[384]{0:T(512)S(1)} %add_rsqrt_fusion.1), kind=kOutput, calls=%fused_computation.167 | convolution fusion | flops 8861515776 | bytes 33302016 | tf_op jit(solution)/shard_map/dot_general | solution.py:689
  91.4 27.0 %multiply_convert_fusion.1 = (bf16[384,5632]{1,0:T(8,128)(2,1)}, bf16[384,5632]{1,0:T(8,128)(2,1)}) fusion(f32[384,5632]{1,0:T(8,128)} %fusion.107, f32[384,5632]{1,0:T(8,128)} %fusion.109, bf16[384,2048]{1,0:T(8,128)(2,1)S(1)} %bitcast.323, bf16[5632,2048]{1,0:T(8,128)(2,1)} %param.28), kind=kOutput, calls=%fused_computation.6 | convolution fusion | flops 8886484992 | bytes 50593792 | tf_op jit(solution)/shard_map/nd,fd->nf/dot_general | solution.py:694
  118.4 16.1 %fusion.114 = f32[384,2048]{1,0:T(8,128)} fusion(bf16[384,5632]{1,0:T(8,128)(2,1)} %get-tuple-element.39, bf16[2048,5632]{1,0:T(8,128)(2,1)} %param.26), kind=kOutput, calls=%fused_computation.171 | convolution fusion | flops 8858370048 | bytes 30539776 | tf_op jit(solution)/shard_map/nf,df->nd/dot_general | solution.py:699
  134.5 17.3 %fusion.24 = (bf16[2048]{0:T(1024)(128)(2,1)S(1)}, f32[384]{0:T(512)S(1)}, f32[384,2048]{1,0:T(8,128)}) fusion(bf16[384,2048]{1,0:T(8,128)(2,1)} %copy-done.23, f32[384]{0:T(512)S(1)} %add_rsqrt_fusion.1, f32[2048]{0:T(1024)S(1)} %convert_element_type.162, f32[384,2048]{1,0:T(8,128)} %fusion.114, bf16[384,5632]{1,0:T(8,128)(2,1)} %get-tuple-element.38, ...), kind=kOutput, calls=%fused_computation.47 | convolution fusion | flops 8864659456 | bytes 35273728 | tf_op jit(solution)/shard_map/nf,df->nd/dot_general | solution.py:700
  151.8 3.8 fusion.23
  157.2 10.1 convolution_convert_fusion.5
  167.3 5.7 reshape.346
  173.0 5.5 copy.52
  178.5 4.9 fusion.59
  183.4 3.7 fusion.74
  187.1 13.5 %fusion.44 = f32[6,4,64,8,64]{4,2,3,1,0:T(8,128)} fusion(bf16[6,64,4,64,1]{1,3,4,2,0:T(8,128)(2,1)S(1)} %copy-done.34, f32[6,4,64,64,8]{3,2,4,1,0:T(8,128)} %fusion.74, f32[6,4,8,64,64]{3,4,2,1,0:T(8,128)} %get-tuple-element.54, f32[6,4,8,64]{3,2,1,0:T(8,128)S(1)} %get-tuple-element.53), kind=kOutput, calls=%fused_computation.79 | convolution fusion | flops 106180672 | bytes 9682944 | tf_op jit(solution)/shard_map/bkgqs,bskd->bqkgd/dot_general | solution.py:710
  200.6 13.0 broadcast_multiply_fusion.1
  213.6 10.4 convolution_convert_fusion.3
  224.0 18.4 %convolution_convert_fusion.2 = bf16[2048,5632]{1,0:T(8,128)(2,1)} fusion(bf16[384,5632]{1,0:T(8,128)(2,1)} %get-tuple-element.39, bf16[384,2048]{1,0:T(8,128)(2,1)S(1)} %copy-done.24, f32[2048]{0:T(1024)S(1)} %convert_element_type.162, f32[384]{0:T(512)S(1)} %add_rsqrt_fusion.1), kind=kOutput, calls=%fused_computation.4 | convolution fusion | flops 8873050112 | bytes 28976640 | tf_op jit(solution)/shard_map/nd,nf->df/dot_general | solution.py:697
  242.4 19.2 %convolution_convert_fusion.1 = bf16[2048,5632]{1,0:T(8,128)(2,1)} fusion(bf16[384,5632]{1,0:T(8,128)(2,1)} %get-tuple-element.38, bf16[384,2048]{1,0:T(8,128)(2,1)} %copy-done.23, f32[2048]{0:T(1024)S(1)} %convert_element_type.162, f32[384]{0:T(512)S(1)} %add_rsqrt_fusion.1), kind=kOutput, calls=%fused_computation.3 | convolution fusion | flops 8873050112 | bytes 28976640 | tf_op jit(solution)/shard_map/nd,nf->df/dot_general | solution.py:698
  261.7 22.2 %convolution_convert_fusion = bf16[5632,2048]{1,0:T(8,128)(2,1)} fusion(bf16[384,2048]{1,0:T(8,128)(2,1)S(1)} %bitcast.324, f32[384,5632]{1,0:T(8,128)} %fusion.109, f32[384,5632]{1,0:T(8,128)} %fusion.107), kind=kOutput, calls=%fused_computation.2 | convolution fusion | flops 8882880512 | bytes 41943040 | tf_op jit(solution)/shard_map/nf,nd->fd/dot_general | solution.py:693
  284.4 3.8 broadcast_multiply_fusion
  288.2 3.5 fusion.111
  291.7 6.1 fusion.7
  297.9 5.3 copy.49
  303.2 5.6 convert_element_type.171
  308.8 8.6 convolution_convert_fusion.4
  317.4 8.6 fusion.115
  331.4 2.9 fusion.34
  334.4 3.4 copy-done.3
  337.7 3.4 copy-done.4
  341.1 55.6 %shard_map.272 = bf16[45056,8,128]{2,1,0:T(8,128)(2,1)} custom-call(bf16[2,8,128]{2,1,0:T(8,128)(2,1)S(1)} %bitcast.309, bf16[4096,8,128]{2,1,0:T(8,128)(2,1)S(1)} %bitcast.303, bf16[512,8,128]{2,1,0:T(8,128)(2,1)S(1)} %bitcast.305, bf16[512,8,128]{2,1,0:T(8,128)(2,1)S(1)} %bitcast.306, bf16[4096,8,128]{2,1,0:T(8,128)(2,1)S(1)} %bitcast.302, ...), custom_call_target="tpu_custom_call" | custom-call | flops 100000000 | bytes 176000000 | tf_op jit(solution)/shard_map/pallas_call | solution.py:559
  396.7 389.3 %shard_map.273 = (bf16[1408,8,128]{2,1,0:T(8,128)(2,1)}, bf16[16,1408,8,128]{3,2,1,0:T(8,128)(2,1)}, bf16[4,3,1408,8,128]{4,3,2,1,0:T(8,128)(2,1)}, bf16[2,4,4,1408,8,128]{5,4,3,2,1,0:T(8,128)(2,1)}) custom-call(bf16[32,1408,8,128]{3,2,1,0:T(8,128)(2,1)} %bitcast.63.src_ref), custom_call_target="tpu_custom_call" | custom-call | tf_op jit(solution)/shard_map/pallas_call | solution.py:518
  788.6 2.7 shard_map.274
  791.3 2.6 copy-done.1
  796.8 18.6 %shard_map.275 = f32[8,128]{1,0:T(8,128)S(1)} custom-call(f32[8,128]{1,0:T(8,128)S(1)} %broadcast_in_dim.20.part_ref), custom_call_target="tpu_custom_call" | custom-call | tf_op jit(solution)/shard_map/pallas_call | solution.py:597
  816.7 15.2 %fusion.64 = (f32[1376384]{0:T(1024)}, f32[10753,128]{1,0:T(8,128)S(1)}, f32[1376384]{0:T(1024)}) fusion(f32[]{:T(128)S(6)} %mul.406, f32[11464,128]{1,0:T(8,128)} %copy-done.1, f32[1376384]{0:T(1024)} %param.31, f32[10753]{0:T(1024)S(1)} %fusion.90, f32[1376384]{0:T(1024)} %param.30, f32[1376384]{0:T(1024)} %param.29), kind=kLoop, calls=%fused_computation.95 | loop fusion | flops 22022144 | bytes 38581768 | tf_op jit(solution)/shard_map/reshape | solution.py:792
  835.8 3.8 shard_map.276.x_ref
  839.6 392.0 %shard_map.277 = bf16[32,1376,8,128]{3,2,1,0:T(8,128)(2,1)} custom-call(bf16[1376,8,128]{2,1,0:T(8,128)(2,1)S(1)} %shard_map.276.x_ref), custom_call_target="tpu_custom_call" | custom-call | tf_op jit(solution)/shard_map/pallas_call | solution.py:322
  1231.6 54.8 %shard_map.278 = (bf16[2,8,128]{2,1,0:T(8,128)(2,1)}, bf16[4096,8,128]{2,1,0:T(8,128)(2,1)S(1)}, bf16[512,8,128]{2,1,0:T(8,128)(2,1)S(1)}, bf16[512,8,128]{2,1,0...) custom-call(bf16[44032,8,128]{2,1,0:T(8,128)(2,1)} %bitcast.72.refs_0_), custom_call_target="tpu_custom_call" | custom-call | flops 100000000 | bytes 176000000 | tf_op jit(solution)/shard_map/pallas_call | solution.py:559
  1286.4 3.3 copy-done.5
  1291.7 20.6 %shard_map.279 = bf16[2048,2048]{1,0:T(8,128)(2,1)} custom-call(bf16[256,16,8,128]{3,2,1,0:T(8,128)(2,1)} %bitcast.304), custom_call_target="tpu_custom_call" | custom-call | flops 4194304 | bytes 16777216 | tf_op jit(solution)/shard_map/pallas_call | solution.py:613
  1312.3 3.6 shard_map.280
  1315.9 3.6 shard_map.281
  (122 shorter events, 31.1 us)
Async XLA Ops:
  0.6 7.9 copy-start
  0.7 7.5 copy-start.9
  3.6 830.8 %collective-permute-start = (f32[3,352,128]{2,1,0:T(8,128)}, f32[3,352,128]{2,1,0:T(8,128)}, u32[]{:S(2)}, u32[]{:S(2)}) collective-permute-start(f32[3,352,128]{2,1,0:T(8,128)} %pad_maximum_fusion), channel_id=1, source_target_pairs={{1,0},{2,1},{3,2},{4,3},{5,4},{6,5},{7,6},{8,7},{9,8},{10,9},{11,1... | collective-permute-start | bytes 1622024 | tf_op jit(solution)/shard_map/ppermute | solution.py:783
  5.7 2.9 copy-start.35
  8.6 1.1 copy-start.25
  10.5 2.9 copy-start.39
  10.5 2.9 copy-start.26
  24.5 3.1 copy-start.16
  24.6 3.1 copy-start.18
  24.8 2.8 copy-start.33
  51.5 7.5 copy-start.38
  59.0 16.5 %copy-start.23 = (bf16[384,2048]{1,0:T(8,128)(2,1)}, bf16[384,2048]{1,0:T(8,128)(2,1)S(1)}, u32[]{:S(2)}) copy-start(bf16[384,2048]{1,0:T(8,128)(2,1)S(1)} %get-tuple-element.56) | copy-start | bytes 4718596
  75.5 15.9 %copy-start.21 = (bf16[6,64,2048]{2,1,0:T(8,128)(2,1)S(1)}, bf16[6,64,2048]{2,1,0:T(8,128)(2,1)}, u32[]{:S(2)}) copy-start(bf16[6,64,2048]{2,1,0:T(8,128)(2,1)} %param.18) | copy-start | bytes 4718596
  155.6 1.6 copy-start.13
  178.5 4.9 copy-start.12
  183.4 3.7 copy-start.34
  187.1 13.5 %copy-start.19 = (f32[6,64,64]{1,2,0:T(8,128)S(1)}, f32[6,64,64]{1,2,0:T(8,128)}, u32[]{:S(2)}) copy-start(f32[6,64,64]{1,2,0:T(8,128)} %copy-done.18) | copy-start | bytes 294916
  213.6 10.5 copy-start.24
  242.4 19.2 %copy-start.22 = (bf16[6,64,2048]{2,1,0:T(8,128)(2,1)S(1)}, bf16[6,64,2048]{2,1,0:T(8,128)(2,1)}, u32[]{:S(2)}) copy-start(bf16[6,64,2048]{2,1,0:T(8,128)(2,1)} %param.18) | copy-start | bytes 4718596
  284.4 7.3 slice-start
  284.4 7.3 slice-start.1
  288.2 3.5 copy-start.17
  297.9 10.9 copy-start.27
  308.8 8.6 copy-start.29
  317.4 8.6 copy-start.32
  317.4 8.7 copy-start.31
  326.0 3.1 copy-start.30
  326.7 2.9 copy-start.28
  329.0 1.4 copy-start.10
  329.1 2.4 copy-start.20
  329.1 2.3 copy-start.36
  329.1 2.3 copy-start.37
  334.4 3.4 copy-start.3
  337.7 3.4 copy-start.4
  786.8 1.8 copy-start.6
  791.3 2.6 copy-start.1
  816.7 15.2 %copy-start.11 = (bf16[6,64,2048]{2,1,0:T(8,128)(2,1)S(1)}, bf16[6,64,2048]{2,1,0:T(8,128)(2,1)}, u32[]{:S(2)}) copy-start(bf16[6,64,2048]{2,1,0:T(8,128)(2,1)} %param.17) | copy-start | bytes 4718596
  816.7 15.2 %copy-start.14 = (f32[384,2048]{1,0:T(8,128)S(1)}, f32[384,2048]{1,0:T(8,128)}, u32[]{:S(2)}) copy-start(f32[384,2048]{1,0:T(8,128)} %copy-done.13) | copy-start | bytes 9437188
  816.7 15.2 %copy-start.15 = (f32[384,2048]{1,0:T(8,128)S(1)}, f32[384,2048]{1,0:T(8,128)}, u32[]{:S(2)}) copy-start(f32[384,2048]{1,0:T(8,128)} %get-tuple-element.60) | copy-start | bytes 9437188
  831.9 3.9 copy-start.2
  1286.4 3.3 copy-start.5
  1289.7 1.0 copy-start.7
  1290.8 1.0 copy-start.8

commit v3 on v2

--- a/solution.py
+++ b/solution.py
@@ -296,14 +296,14 @@
     beside(1)
     across(0)
     column(3)
+    planes(1)
     beside(2)
+    planes(2)
     across(1)
-    planes(1)
     beside(3)
     across(2)
-    planes(2)
+    planes(3)
     across(3)
-    planes(3)
 
     def drain(k, carry):
         for part in (ONE, TWO, SMALLS):
@@ -466,7 +466,6 @@
             enter(k, *HERE, part, True)
             collect(k, *HERE, part)
             if k < 3:
-                sent.append((along(k, *HERE, part, 0)[2], part))
                 pass_on(k, *HERE, part)
 
     small(0)
@@ -480,23 +479,27 @@
     prepare(2)
     chain(1)
     second(1)
+    second(2)
     chain(2)
     prepare(3)
+    for k in range(3):
+        for part in (ONE, TWO):
+            sent.append((along(k, *HERE, part, 0)[2], part))
+    pl.when(is_end)(lambda: final(0))
     for piece in smalls:
         collect(3, *piece)
-    for dy, dx, part in ((*BY_XY, SMALL_ONE), (*BY_XY, SMALL_TWO), (*BY_Y, SMALL_ONE), (*BY_X, SMALL_TWO)):
-        leave(3, dy, dx, part)
-    final(0)
+    for piece in ((*BY_XY, SMALL_ONE), (*BY_XY, SMALL_TWO), (*BY_Y, SMALL_ONE), (*BY_X, SMALL_TWO)):
+        leave(3, *piece)
+    pl.when(jnp.logical_not(is_end))(lambda: final(0))
+    final(1)
+    second(3)
+    final(2)
     for piece in ((*BY_X, SMALL_ONE), (*BY_Y, SMALL_TWO)):
         enter(3, *piece)
         leave(3, *piece, True)
-    second(2)
-    final(1)
-    second(3)
     for part in (SMALL_ONE, SMALL_TWO):
         enter(3, *HERE, part)
         enter(3, *HERE, part, True)
-    final(2)
     final(3)
     out = pltpu.make_async_copy(acc.at[12], out_ref, out_sem)
     out.start()

time: 1330 us -> 1220 us (0.917)
  Pallas kernels: 945 us -> 832 us
    pallas_call x1, Pallas kernels: 392 us -> 312 us  [gather(): pl.pallas_call(gather_kernel, out_shape=jax.ShapeDtypeStruct((NDEV, WIN_A...]
    pallas_call x1, Pallas kernels: 389 us -> 359 us  [scatter(): pl.pallas_call(scatter_kernel, out_shape=(lands(), lands(16), lands(4, 3)...]
  transfers between devices with their start and end apart: 1 -> 1, of which waited for: 0 -> 0; matrix products, arithmetic and copies ran while one was open for 26% -> 29% of each run, Pallas kernels for 35% -> 36%
where the time goes in v3:
time: 1220 us; the launch traced here: 1210 us
  Pallas kernels  832 us (68%)
  matrix products  265 us (22%)
  local copies, waits for them, and re-layouts  59.5 us (5%)
  other arithmetic  47.2 us (4%)
    pallas_call x1, Pallas kernels, scatter(): pl.pallas_call(scatter_kernel, out_shape=(lands(), lands(16), lands(4, 3)...  359 us
    pallas_call x1, Pallas kernels, gather(): pl.pallas_call(gather_kernel, out_shape=jax.ShapeDtypeStruct((NDEV, WIN_A...  312 us
    pallas_call x2, Pallas kernels, move(): pl.pallas_call(functools.partial(move_kernel, moves, len(arrays), len(out...  110 us
    pallas_call x3, Pallas kernels, turned(): pl.pallas_call(turn_kernel, out_shape=jax.ShapeDtypeStruct((cols, rows),...  27.8 us
    dot_general x1, matrix products, local_grads(): jnp.einsum('nd,fd->nf', dy_flat, w_down, preferred_element_type=F32)  27 us
  transfers between devices with their start and end apart: 1, of which 0 were waited for; matrix products, arithmetic and copies ran while one was open for 29% of the time, Pallas kernels for 36%

profile of v3, /device:TPU:0, one launch (start us, length us, event | category | flops | bytes accessed | tf_op | source)
XLA Modules:
  0.0 1208.6 jit_solution(6454137996282869385)
XLA Ops:
  10.6 2.8 fusion.46
  13.5 9.5 fusion.3
  24.8 2.8 fusion.6
  27.6 7.1 fusion.113
  34.7 5.5 convert_bitcast_fusion
  40.2 5.2 copy.45
  45.4 6.1 reshape.343
  51.6 7.5 fusion.25
  59.0 16.4 %fusion.107 = f32[384,5632]{1,0:T(8,128)} fusion(bf16[2048,5632]{1,0:T(8,128)(2,1)} %param.26, bf16[384,2048]{1,0:T(8,128)(2,1)S(1)} %get-tuple-element.56, f32[2048]{0:T(1024)S(1)} %convert_element_type.162, f32[384]{0:T(512)S(1)} %add_rsqrt_fusion.1), kind=kOutput, calls=%fused_computation.166 | convolution fusion | flops 8861515776 | bytes 33302016 | tf_op jit(solution)/shard_map/dot_general | solution.py:691
  75.5 15.9 %fusion.109 = f32[384,5632]{1,0:T(8,128)} fusion(bf16[2048,5632]{1,0:T(8,128)(2,1)} %param.27, bf16[384,2048]{1,0:T(8,128)(2,1)S(1)} %get-tuple-element.56, f32[2048]{0:T(1024)S(1)} %convert_element_type.162, f32[384]{0:T(512)S(1)} %add_rsqrt_fusion.1), kind=kOutput, calls=%fused_computation.167 | convolution fusion | flops 8861515776 | bytes 33302016 | tf_op jit(solution)/shard_map/dot_general | solution.py:692
  91.4 27.0 %multiply_convert_fusion.1 = (bf16[384,5632]{1,0:T(8,128)(2,1)}, bf16[384,5632]{1,0:T(8,128)(2,1)}) fusion(f32[384,5632]{1,0:T(8,128)} %fusion.107, f32[384,5632]{1,0:T(8,128)} %fusion.109, bf16[384,2048]{1,0:T(8,128)(2,1)S(1)} %bitcast.323, bf16[5632,2048]{1,0:T(8,128)(2,1)} %param.28), kind=kOutput, calls=%fused_computation.6 | convolution fusion | flops 8886484992 | bytes 50593792 | tf_op jit(solution)/shard_map/nd,fd->nf/dot_general | solution.py:697
  118.4 16.1 %fusion.114 = f32[384,2048]{1,0:T(8,128)} fusion(bf16[384,5632]{1,0:T(8,128)(2,1)} %get-tuple-element.39, bf16[2048,5632]{1,0:T(8,128)(2,1)} %param.26), kind=kOutput, calls=%fused_computation.171 | convolution fusion | flops 8858370048 | bytes 30539776 | tf_op jit(solution)/shard_map/nf,df->nd/dot_general | solution.py:702
  134.5 17.3 %fusion.24 = (bf16[2048]{0:T(1024)(128)(2,1)S(1)}, f32[384]{0:T(512)S(1)}, f32[384,2048]{1,0:T(8,128)}) fusion(bf16[384,2048]{1,0:T(8,128)(2,1)} %copy-done.23, f32[384]{0:T(512)S(1)} %add_rsqrt_fusion.1, f32[2048]{0:T(1024)S(1)} %convert_element_type.162, f32[384,2048]{1,0:T(8,128)} %fusion.114, bf16[384,5632]{1,0:T(8,128)(2,1)} %get-tuple-element.38, ...), kind=kOutput, calls=%fused_computation.47 | convolution fusion | flops 8864659456 | bytes 35273728 | tf_op jit(solution)/shard_map/nf,df->nd/dot_general | solution.py:703
  151.8 3.8 fusion.23
  157.2 10.1 convolution_convert_fusion.5
  167.3 5.7 reshape.346
  173.0 5.5 copy.52
  178.5 4.9 fusion.59
  183.4 3.7 fusion.74
  187.1 13.5 %fusion.44 = f32[6,4,64,8,64]{4,2,3,1,0:T(8,128)} fusion(bf16[6,64,4,64,1]{1,3,4,2,0:T(8,128)(2,1)S(1)} %copy-done.34, f32[6,4,64,64,8]{3,2,4,1,0:T(8,128)} %fusion.74, f32[6,4,8,64,64]{3,4,2,1,0:T(8,128)} %get-tuple-element.54, f32[6,4,8,64]{3,2,1,0:T(8,128)S(1)} %get-tuple-element.53), kind=kOutput, calls=%fused_computation.79 | convolution fusion | flops 106180672 | bytes 9682944 | tf_op jit(solution)/shard_map/bkgqs,bskd->bqkgd/dot_general | solution.py:713
  200.6 13.0 %broadcast_multiply_fusion.1 = (f32[6,64,4,64]{1,3,2,0:T(8,128)}, f32[6,64,4,64]{1,3,2,0:T(8,128)}) fusion(f32[6,64,64]{1,2,0:T(8,128)S(1)} %copy-done.19, bf16[6,64,4,8,64]{1,4,3,2,0:T(8,128)(2,1)} %bitcast.320, f32[6,4,64,64,8]{3,2,4,1,0:T(8,128)} %fusion.74, f32[6,4,8,64,64]{3,4,2,1,0:T(8,128)} %get-tuple-element.54, ...), kind=kOutput, calls=%fused_computation.108 | convolution fusion | flops 106278976 | bytes 8798208 | tf_op jit(solution)/shard_map/bkgqs,bqkgd->bskd/dot_general | solution.py:714
  213.6 10.4 convolution_convert_fusion.3
  224.0 18.4 %convolution_convert_fusion.2 = bf16[2048,5632]{1,0:T(8,128)(2,1)} fusion(bf16[384,5632]{1,0:T(8,128)(2,1)} %get-tuple-element.39, bf16[384,2048]{1,0:T(8,128)(2,1)S(1)} %copy-done.24, f32[2048]{0:T(1024)S(1)} %convert_element_type.162, f32[384]{0:T(512)S(1)} %add_rsqrt_fusion.1), kind=kOutput, calls=%fused_computation.4 | convolution fusion | flops 8873050112 | bytes 28976640 | tf_op jit(solution)/shard_map/nd,nf->df/dot_general | solution.py:700
  242.4 19.2 %convolution_convert_fusion.1 = bf16[2048,5632]{1,0:T(8,128)(2,1)} fusion(bf16[384,5632]{1,0:T(8,128)(2,1)} %get-tuple-element.38, bf16[384,2048]{1,0:T(8,128)(2,1)} %copy-done.23, f32[2048]{0:T(1024)S(1)} %convert_element_type.162, f32[384]{0:T(512)S(1)} %add_rsqrt_fusion.1), kind=kOutput, calls=%fused_computation.3 | convolution fusion | flops 8873050112 | bytes 28976640 | tf_op jit(solution)/shard_map/nd,nf->df/dot_general | solution.py:701
  261.7 22.2 %convolution_convert_fusion = bf16[5632,2048]{1,0:T(8,128)(2,1)} fusion(bf16[384,2048]{1,0:T(8,128)(2,1)S(1)} %bitcast.324, f32[384,5632]{1,0:T(8,128)} %fusion.109, f32[384,5632]{1,0:T(8,128)} %fusion.107), kind=kOutput, calls=%fused_computation.2 | convolution fusion | flops 8882880512 | bytes 41943040 | tf_op jit(solution)/shard_map/nf,nd->fd/dot_general | solution.py:696
  284.4 3.8 broadcast_multiply_fusion
  288.2 3.5 fusion.111
  291.7 6.1 fusion.7
  297.9 5.3 copy.49
  303.2 5.6 convert_element_type.171
  308.8 8.6 convolution_convert_fusion.4
  317.4 8.6 fusion.115
  331.4 2.9 fusion.34
  334.4 3.4 copy-done.3
  337.7 3.4 copy-done.4
  341.1 55.6 %shard_map.272 = bf16[45056,8,128]{2,1,0:T(8,128)(2,1)} custom-call(bf16[2,8,128]{2,1,0:T(8,128)(2,1)S(1)} %bitcast.309, bf16[4096,8,128]{2,1,0:T(8,128)(2,1)S(1)} %bitcast.303, bf16[512,8,128]{2,1,0:T(8,128)(2,1)S(1)} %bitcast.305, bf16[512,8,128]{2,1,0:T(8,128)(2,1)S(1)} %bitcast.306, bf16[4096,8,128]{2,1,0:T(8,128)(2,1)S(1)} %bitcast.302, ...), custom_call_target="tpu_custom_call" | custom-call | flops 100000000 | bytes 176000000 | tf_op jit(solution)/shard_map/pallas_call | solution.py:562
  396.7 359.4 %shard_map.273 = (bf16[1408,8,128]{2,1,0:T(8,128)(2,1)}, bf16[16,1408,8,128]{3,2,1,0:T(8,128)(2,1)}, bf16[4,3,1408,8,128]{4,3,2,1,0:T(8,128)(2,1)}, bf16[2,4,4,1408,8,128]{5,4,3,2,1,0:T(8,128)(2,1)}) custom-call(bf16[32,1408,8,128]{3,2,1,0:T(8,128)(2,1)} %bitcast.63.src_ref), custom_call_target="tpu_custom_call" | custom-call | tf_op jit(solution)/shard_map/pallas_call | solution.py:521
  758.7 2.7 shard_map.274
  761.4 2.6 copy-done.1
  766.9 16.0 %shard_map.275 = f32[8,128]{1,0:T(8,128)S(1)} custom-call(f32[8,128]{1,0:T(8,128)S(1)} %broadcast_in_dim.20.part_ref), custom_call_target="tpu_custom_call" | custom-call | tf_op jit(solution)/shard_map/pallas_call | solution.py:600
  784.2 15.2 %fusion.64 = (f32[1376384]{0:T(1024)}, f32[10753,128]{1,0:T(8,128)S(1)}, f32[1376384]{0:T(1024)}) fusion(f32[]{:T(128)S(6)} %mul.406, f32[11464,128]{1,0:T(8,128)} %copy-done.1, f32[1376384]{0:T(1024)} %param.31, f32[10753]{0:T(1024)S(1)} %fusion.90, f32[1376384]{0:T(1024)} %param.30, f32[1376384]{0:T(1024)} %param.29), kind=kLoop, calls=%fused_computation.95 | loop fusion | flops 22022144 | bytes 38581768 | tf_op jit(solution)/shard_map/reshape | solution.py:795
  803.3 3.8 shard_map.276.x_ref
  807.2 312.0 %shard_map.277 = bf16[32,1376,8,128]{3,2,1,0:T(8,128)(2,1)} custom-call(bf16[1376,8,128]{2,1,0:T(8,128)(2,1)S(1)} %shard_map.276.x_ref), custom_call_target="tpu_custom_call" | custom-call | tf_op jit(solution)/shard_map/pallas_call | solution.py:322
  1119.2 54.8 %shard_map.278 = (bf16[2,8,128]{2,1,0:T(8,128)(2,1)}, bf16[4096,8,128]{2,1,0:T(8,128)(2,1)S(1)}, bf16[512,8,128]{2,1,0:T(8,128)(2,1)S(1)}, bf16[512,8,128]{2,1,0...) custom-call(bf16[44032,8,128]{2,1,0:T(8,128)(2,1)} %bitcast.72.refs_0_), custom_call_target="tpu_custom_call" | custom-call | flops 100000000 | bytes 176000000 | tf_op jit(solution)/shard_map/pallas_call | solution.py:562
  1174.1 3.3 copy-done.5
  1179.4 20.6 %shard_map.279 = bf16[2048,2048]{1,0:T(8,128)(2,1)} custom-call(bf16[256,16,8,128]{3,2,1,0:T(8,128)(2,1)} %bitcast.304), custom_call_target="tpu_custom_call" | custom-call | flops 4194304 | bytes 16777216 | tf_op jit(solution)/shard_map/pallas_call | solution.py:616
  1200.0 3.6 shard_map.280
  1203.6 3.6 shard_map.281
  (122 shorter events, 31.1 us)
Async XLA Ops:
  0.6 7.9 copy-start
  0.7 7.5 copy-start.9
  3.6 798.3 %collective-permute-start = (f32[3,352,128]{2,1,0:T(8,128)}, f32[3,352,128]{2,1,0:T(8,128)}, u32[]{:S(2)}, u32[]{:S(2)}) collective-permute-start(f32[3,352,128]{2,1,0:T(8,128)} %pad_maximum_fusion), channel_id=1, source_target_pairs={{1,0},{2,1},{3,2},{4,3},{5,4},{6,5},{7,6},{8,7},{9,8},{10,9},{11,1... | collective-permute-start | bytes 1622024 | tf_op jit(solution)/shard_map/ppermute | solution.py:786
  5.7 2.9 copy-start.35
  8.6 1.1 copy-start.25
  10.5 2.9 copy-start.39
  10.5 2.9 copy-start.26
  24.5 3.1 copy-start.16
  24.6 3.1 copy-start.18
  24.8 2.8 copy-start.33
  51.5 7.5 copy-start.38
  59.0 16.5 %copy-start.23 = (bf16[384,2048]{1,0:T(8,128)(2,1)}, bf16[384,2048]{1,0:T(8,128)(2,1)S(1)}, u32[]{:S(2)}) copy-start(bf16[384,2048]{1,0:T(8,128)(2,1)S(1)} %get-tuple-element.56) | copy-start | bytes 4718596
  75.5 15.9 %copy-start.21 = (bf16[6,64,2048]{2,1,0:T(8,128)(2,1)S(1)}, bf16[6,64,2048]{2,1,0:T(8,128)(2,1)}, u32[]{:S(2)}) copy-start(bf16[6,64,2048]{2,1,0:T(8,128)(2,1)} %param.18) | copy-start | bytes 4718596
  155.6 1.6 copy-start.13
  178.5 4.9 copy-start.12
  183.4 3.7 copy-start.34
  187.1 13.5 %copy-start.19 = (f32[6,64,64]{1,2,0:T(8,128)S(1)}, f32[6,64,64]{1,2,0:T(8,128)}, u32[]{:S(2)}) copy-start(f32[6,64,64]{1,2,0:T(8,128)} %copy-done.18) | copy-start | bytes 294916
  213.6 10.5 copy-start.24
  242.4 19.2 %copy-start.22 = (bf16[6,64,2048]{2,1,0:T(8,128)(2,1)S(1)}, bf16[6,64,2048]{2,1,0:T(8,128)(2,1)}, u32[]{:S(2)}) copy-start(bf16[6,64,2048]{2,1,0:T(8,128)(2,1)} %param.18) | copy-start | bytes 4718596
  284.4 7.3 slice-start
  284.4 7.3 slice-start.1
  288.2 3.5 copy-start.17
  297.9 10.9 copy-start.27
  308.8 8.6 copy-start.29
  317.4 8.6 copy-start.32
  317.4 8.7 copy-start.31
  326.0 3.1 copy-start.30
  326.7 2.9 copy-start.28
  329.0 1.4 copy-start.10
  329.1 2.4 copy-start.20
  329.1 2.3 copy-start.36
  329.1 2.3 copy-start.37
  334.4 3.4 copy-start.3
  337.7 3.4 copy-start.4
  756.9 1.8 copy-start.6
  761.4 2.6 copy-start.1
  784.2 15.2 %copy-start.11 = (bf16[6,64,2048]{2,1,0:T(8,128)(2,1)S(1)}, bf16[6,64,2048]{2,1,0:T(8,128)(2,1)}, u32[]{:S(2)}) copy-start(bf16[6,64,2048]{2,1,0:T(8,128)(2,1)} %param.17) | copy-start | bytes 4718596
  784.2 15.2 %copy-start.14 = (f32[384,2048]{1,0:T(8,128)S(1)}, f32[384,2048]{1,0:T(8,128)}, u32[]{:S(2)}) copy-start(f32[384,2048]{1,0:T(8,128)} %copy-done.13) | copy-start | bytes 9437188
  784.2 15.2 %copy-start.15 = (f32[384,2048]{1,0:T(8,128)S(1)}, f32[384,2048]{1,0:T(8,128)}, u32[]{:S(2)}) copy-start(f32[384,2048]{1,0:T(8,128)} %get-tuple-element.60) | copy-start | bytes 9437188
  799.4 3.9 copy-start.2
  1174.1 3.3 copy-start.5
  1177.3 1.0 copy-start.7
  1178.4 1.0 copy-start.8

commit v4 on v3

--- a/solution.py
+++ b/solution.py
@@ -607,18 +607,24 @@
     return total[0, 0]
 
 
+TURN = 512
+
+
 def turn_kernel(x_ref, o_ref):
-    rows = x_ref.shape[0] * 8
-    o_ref[...] = x_ref[...].astype(F32).reshape(rows, LANES).T.astype(jnp.bfloat16)
+    for c in range(o_ref.shape[0] // LANES):
+        for r in range(o_ref.shape[1] // TURN):
+            x = x_ref[r * (TURN // SUB):(r + 1) * (TURN // SUB), c].astype(F32).reshape(TURN, LANES)
+            o_ref[c * LANES:(c + 1) * LANES, r * TURN:(r + 1) * TURN] = x.T.astype(jnp.bfloat16)
 
 
 def turned(tiles, rows, cols):
+    wide = min(cols, 2 * LANES)
     return pl.pallas_call(
         turn_kernel,
         out_shape=jax.ShapeDtypeStruct((cols, rows), jnp.bfloat16),
-        grid=(cols // LANES, rows // 1024),
-        in_specs=[pl.BlockSpec((LANES, None, SUB, LANES), lambda j, i: (i, j, 0, 0))],
-        out_specs=pl.BlockSpec((LANES, 1024), lambda j, i: (j, i)),
+        grid=(cols // wide,),
+        in_specs=[pl.BlockSpec((rows // SUB, wide // LANES, SUB, LANES), lambda j: (0, j, 0, 0))],
+        out_specs=pl.BlockSpec((wide, rows), lambda j: (j, 0)),
         cost_estimate=pl.CostEstimate(flops=rows * cols, bytes_accessed=4 * rows * cols, transcendentals=0),
     )(tiles.reshape(rows // SUB, cols // LANES, SUB, LANES))
 

time: 1220 us -> 1200 us (0.984)
    pallas_call x3, Pallas kernels: 27.8 us -> 15.1 us  [turned(): pl.pallas_call(turn_kernel, out_shape=jax.ShapeDtypeStruct((cols, rows),...]
where the time goes in v4:
time: 1200 us
  Pallas kernels  820 us (68%)
  matrix products  265 us (22%)
  local copies, waits for them, and re-layouts  59.5 us (5%)
  other arithmetic  47.2 us (4%)
    pallas_call x1, Pallas kernels, scatter(): pl.pallas_call(scatter_kernel, out_shape=(lands(), lands(16), lands(4, 3)...  359 us
    pallas_call x1, Pallas kernels, gather(): pl.pallas_call(gather_kernel, out_shape=jax.ShapeDtypeStruct((NDEV, WIN_A...  312 us
    pallas_call x2, Pallas kernels, move(): pl.pallas_call(functools.partial(move_kernel, moves, len(arrays), len(out...  110 us
    dot_general x1, matrix products, local_grads(): jnp.einsum('nd,fd->nf', dy_flat, w_down, preferred_element_type=F32)  27 us
  transfers between devices with their start and end apart: 1, of which 0 were waited for; matrix products, arithmetic and copies ran while one was open for 29% of the time, Pallas kernels for 36%

profile of v4, /device:TPU:0, one launch (start us, length us, event | category | flops | bytes accessed | tf_op | source)
XLA Modules:
  0.0 1195.9 jit_solution(9044497456818232480)
XLA Ops:
  10.6 2.8 fusion.46
  13.5 9.5 fusion.3
  24.8 2.8 fusion.6
  27.6 7.1 fusion.113
  34.7 5.5 convert_bitcast_fusion
  40.2 5.2 copy.45
  45.4 6.1 reshape.343
  51.6 7.5 fusion.25
  59.0 16.4 %fusion.107 = f32[384,5632]{1,0:T(8,128)} fusion(bf16[2048,5632]{1,0:T(8,128)(2,1)} %param.26, bf16[384,2048]{1,0:T(8,128)(2,1)S(1)} %get-tuple-element.56, f32[2048]{0:T(1024)S(1)} %convert_element_type.162, f32[384]{0:T(512)S(1)} %add_rsqrt_fusion.1), kind=kOutput, calls=%fused_computation.166 | convolution fusion | flops 8861515776 | bytes 33302016 | tf_op jit(solution)/shard_map/dot_general | solution.py:697
  75.5 15.9 %fusion.109 = f32[384,5632]{1,0:T(8,128)} fusion(bf16[2048,5632]{1,0:T(8,128)(2,1)} %param.27, bf16[384,2048]{1,0:T(8,128)(2,1)S(1)} %get-tuple-element.56, f32[2048]{0:T(1024)S(1)} %convert_element_type.162, f32[384]{0:T(512)S(1)} %add_rsqrt_fusion.1), kind=kOutput, calls=%fused_computation.167 | convolution fusion | flops 8861515776 | bytes 33302016 | tf_op jit(solution)/shard_map/dot_general | solution.py:698
  91.4 27.0 %multiply_convert_fusion.1 = (bf16[384,5632]{1,0:T(8,128)(2,1)}, bf16[384,5632]{1,0:T(8,128)(2,1)}) fusion(f32[384,5632]{1,0:T(8,128)} %fusion.107, f32[384,5632]{1,0:T(8,128)} %fusion.109, bf16[384,2048]{1,0:T(8,128)(2,1)S(1)} %bitcast.323, bf16[5632,2048]{1,0:T(8,128)(2,1)} %param.28), kind=kOutput, calls=%fused_computation.6 | convolution fusion | flops 8886484992 | bytes 50593792 | tf_op jit(solution)/shard_map/nd,fd->nf/dot_general | solution.py:703
  118.4 16.1 %fusion.114 = f32[384,2048]{1,0:T(8,128)} fusion(bf16[384,5632]{1,0:T(8,128)(2,1)} %get-tuple-element.39, bf16[2048,5632]{1,0:T(8,128)(2,1)} %param.26), kind=kOutput, calls=%fused_computation.171 | convolution fusion | flops 8858370048 | bytes 30539776 | tf_op jit(solution)/shard_map/nf,df->nd/dot_general | solution.py:708
  134.5 17.3 %fusion.24 = (bf16[2048]{0:T(1024)(128)(2,1)S(1)}, f32[384]{0:T(512)S(1)}, f32[384,2048]{1,0:T(8,128)}) fusion(bf16[384,2048]{1,0:T(8,128)(2,1)} %copy-done.23, f32[384]{0:T(512)S(1)} %add_rsqrt_fusion.1, f32[2048]{0:T(1024)S(1)} %convert_element_type.162, f32[384,2048]{1,0:T(8,128)} %fusion.114, bf16[384,5632]{1,0:T(8,128)(2,1)} %get-tuple-element.38, ...), kind=kOutput, calls=%fused_computation.47 | convolution fusion | flops 8864659456 | bytes 35273728 | tf_op jit(solution)/shard_map/nf,df->nd/dot_general | solution.py:709
  151.8 3.8 fusion.23
  157.2 10.1 convolution_convert_fusion.5
  167.3 5.7 reshape.346
  173.0 5.5 copy.52
  178.5 4.9 fusion.59
  183.4 3.7 fusion.74
  187.1 13.5 %fusion.44 = f32[6,4,64,8,64]{4,2,3,1,0:T(8,128)} fusion(bf16[6,64,4,64,1]{1,3,4,2,0:T(8,128)(2,1)S(1)} %copy-done.34, f32[6,4,64,64,8]{3,2,4,1,0:T(8,128)} %fusion.74, f32[6,4,8,64,64]{3,4,2,1,0:T(8,128)} %get-tuple-element.54, f32[6,4,8,64]{3,2,1,0:T(8,128)S(1)} %get-tuple-element.53), kind=kOutput, calls=%fused_computation.79 | convolution fusion | flops 106180672 | bytes 9682944 | tf_op jit(solution)/shard_map/bkgqs,bskd->bqkgd/dot_general | solution.py:719
  200.6 13.0 %broadcast_multiply_fusion.1 = (f32[6,64,4,64]{1,3,2,0:T(8,128)}, f32[6,64,4,64]{1,3,2,0:T(8,128)}) fusion(f32[6,64,64]{1,2,0:T(8,128)S(1)} %copy-done.19, bf16[6,64,4,8,64]{1,4,3,2,0:T(8,128)(2,1)} %bitcast.320, f32[6,4,64,64,8]{3,2,4,1,0:T(8,128)} %fusion.74, f32[6,4,8,64,64]{3,4,2,1,0:T(8,128)} %get-tuple-element.54, ...), kind=kOutput, calls=%fused_computation.108 | convolution fusion | flops 106278976 | bytes 8798208 | tf_op jit(solution)/shard_map/bkgqs,bqkgd->bskd/dot_general | solution.py:720
  213.6 10.4 convolution_convert_fusion.3
  224.0 18.4 %convolution_convert_fusion.2 = bf16[2048,5632]{1,0:T(8,128)(2,1)} fusion(bf16[384,5632]{1,0:T(8,128)(2,1)} %get-tuple-element.39, bf16[384,2048]{1,0:T(8,128)(2,1)S(1)} %copy-done.24, f32[2048]{0:T(1024)S(1)} %convert_element_type.162, f32[384]{0:T(512)S(1)} %add_rsqrt_fusion.1), kind=kOutput, calls=%fused_computation.4 | convolution fusion | flops 8873050112 | bytes 28976640 | tf_op jit(solution)/shard_map/nd,nf->df/dot_general | solution.py:706
  242.4 19.2 %convolution_convert_fusion.1 = bf16[2048,5632]{1,0:T(8,128)(2,1)} fusion(bf16[384,5632]{1,0:T(8,128)(2,1)} %get-tuple-element.38, bf16[384,2048]{1,0:T(8,128)(2,1)} %copy-done.23, f32[2048]{0:T(1024)S(1)} %convert_element_type.162, f32[384]{0:T(512)S(1)} %add_rsqrt_fusion.1), kind=kOutput, calls=%fused_computation.3 | convolution fusion | flops 8873050112 | bytes 28976640 | tf_op jit(solution)/shard_map/nd,nf->df/dot_general | solution.py:707
  261.7 22.2 %convolution_convert_fusion = bf16[5632,2048]{1,0:T(8,128)(2,1)} fusion(bf16[384,2048]{1,0:T(8,128)(2,1)S(1)} %bitcast.324, f32[384,5632]{1,0:T(8,128)} %fusion.109, f32[384,5632]{1,0:T(8,128)} %fusion.107), kind=kOutput, calls=%fused_computation.2 | convolution fusion | flops 8882880512 | bytes 41943040 | tf_op jit(solution)/shard_map/nf,nd->fd/dot_general | solution.py:702
  284.4 3.8 broadcast_multiply_fusion
  288.2 3.5 fusion.111
  291.7 6.1 fusion.7
  297.9 5.3 copy.49
  303.2 5.6 convert_element_type.171
  308.8 8.6 convolution_convert_fusion.4
  317.4 8.6 fusion.115
  331.4 2.9 fusion.34
  334.4 3.4 copy-done.3
  337.7 3.4 copy-done.4
  341.1 55.6 %shard_map.272 = bf16[45056,8,128]{2,1,0:T(8,128)(2,1)} custom-call(bf16[2,8,128]{2,1,0:T(8,128)(2,1)S(1)} %bitcast.309, bf16[4096,8,128]{2,1,0:T(8,128)(2,1)S(1)} %bitcast.303, bf16[512,8,128]{2,1,0:T(8,128)(2,1)S(1)} %bitcast.305, bf16[512,8,128]{2,1,0:T(8,128)(2,1)S(1)} %bitcast.306, bf16[4096,8,128]{2,1,0:T(8,128)(2,1)S(1)} %bitcast.302, ...), custom_call_target="tpu_custom_call" | custom-call | flops 100000000 | bytes 176000000 | tf_op jit(solution)/shard_map/pallas_call | solution.py:562
  396.7 359.4 %shard_map.273 = (bf16[1408,8,128]{2,1,0:T(8,128)(2,1)}, bf16[16,1408,8,128]{3,2,1,0:T(8,128)(2,1)}, bf16[4,3,1408,8,128]{4,3,2,1,0:T(8,128)(2,1)}, bf16[2,4,4,1408,8,128]{5,4,3,2,1,0:T(8,128)(2,1)}) custom-call(bf16[32,1408,8,128]{3,2,1,0:T(8,128)(2,1)} %bitcast.63.src_ref), custom_call_target="tpu_custom_call" | custom-call | tf_op jit(solution)/shard_map/pallas_call | solution.py:521
  758.7 2.7 shard_map.274
  761.4 2.6 copy-done.1
  766.9 16.0 %shard_map.275 = f32[8,128]{1,0:T(8,128)S(1)} custom-call(f32[8,128]{1,0:T(8,128)S(1)} %broadcast_in_dim.20.part_ref), custom_call_target="tpu_custom_call" | custom-call | tf_op jit(solution)/shard_map/pallas_call | solution.py:600
  784.2 15.2 %fusion.64 = (f32[1376384]{0:T(1024)}, f32[10753,128]{1,0:T(8,128)S(1)}, f32[1376384]{0:T(1024)}) fusion(f32[]{:T(128)S(6)} %mul.406, f32[11464,128]{1,0:T(8,128)} %copy-done.1, f32[1376384]{0:T(1024)} %param.31, f32[10753]{0:T(1024)S(1)} %fusion.90, f32[1376384]{0:T(1024)} %param.30, f32[1376384]{0:T(1024)} %param.29), kind=kLoop, calls=%fused_computation.95 | loop fusion | flops 22022144 | bytes 38581768 | tf_op jit(solution)/shard_map/reshape | solution.py:801
  803.3 3.8 shard_map.276.x_ref
  807.2 312.0 %shard_map.277 = bf16[32,1376,8,128]{3,2,1,0:T(8,128)(2,1)} custom-call(bf16[1376,8,128]{2,1,0:T(8,128)(2,1)S(1)} %shard_map.276.x_ref), custom_call_target="tpu_custom_call" | custom-call | tf_op jit(solution)/shard_map/pallas_call | solution.py:322
  1119.2 54.8 %shard_map.278 = (bf16[2,8,128]{2,1,0:T(8,128)(2,1)}, bf16[4096,8,128]{2,1,0:T(8,128)(2,1)S(1)}, bf16[512,8,128]{2,1,0:T(8,128)(2,1)S(1)}, bf16[512,8,128]{2,1,0...) custom-call(bf16[44032,8,128]{2,1,0:T(8,128)(2,1)} %bitcast.72.refs_0_), custom_call_target="tpu_custom_call" | custom-call | flops 100000000 | bytes 176000000 | tf_op jit(solution)/shard_map/pallas_call | solution.py:562
  1174.1 3.3 copy-done.5
  1179.4 10.1 shard_map.279
  1189.4 2.5 shard_map.280
  1192.0 2.5 shard_map.281
  (122 shorter events, 31.1 us)
Async XLA Ops:
  0.6 7.9 copy-start
  0.7 7.5 copy-start.9
  3.6 798.3 %collective-permute-start = (f32[3,352,128]{2,1,0:T(8,128)}, f32[3,352,128]{2,1,0:T(8,128)}, u32[]{:S(2)}, u32[]{:S(2)}) collective-permute-start(f32[3,352,128]{2,1,0:T(8,128)} %pad_maximum_fusion), channel_id=1, source_target_pairs={{1,0},{2,1},{3,2},{4,3},{5,4},{6,5},{7,6},{8,7},{9,8},{10,9},{11,1... | collective-permute-start | bytes 1622024 | tf_op jit(solution)/shard_map/ppermute | solution.py:792
  5.7 2.9 copy-start.35
  8.6 1.1 copy-start.25
  10.5 2.9 copy-start.39
  10.5 2.9 copy-start.26
  24.5 3.1 copy-start.16
  24.6 3.1 copy-start.18
  24.8 2.8 copy-start.33
  51.5 7.5 copy-start.38
  59.0 16.5 %copy-start.23 = (bf16[384,2048]{1,0:T(8,128)(2,1)}, bf16[384,2048]{1,0:T(8,128)(2,1)S(1)}, u32[]{:S(2)}) copy-start(bf16[384,2048]{1,0:T(8,128)(2,1)S(1)} %get-tuple-element.56) | copy-start | bytes 4718596
  75.5 15.9 %copy-start.21 = (bf16[6,64,2048]{2,1,0:T(8,128)(2,1)S(1)}, bf16[6,64,2048]{2,1,0:T(8,128)(2,1)}, u32[]{:S(2)}) copy-start(bf16[6,64,2048]{2,1,0:T(8,128)(2,1)} %param.18) | copy-start | bytes 4718596
  155.6 1.6 copy-start.13
  178.5 4.9 copy-start.12
  183.4 3.7 copy-start.34
  187.1 13.5 %copy-start.19 = (f32[6,64,64]{1,2,0:T(8,128)S(1)}, f32[6,64,64]{1,2,0:T(8,128)}, u32[]{:S(2)}) copy-start(f32[6,64,64]{1,2,0:T(8,128)} %copy-done.18) | copy-start | bytes 294916
  213.6 10.5 copy-start.24
  242.4 19.2 %copy-start.22 = (bf16[6,64,2048]{2,1,0:T(8,128)(2,1)S(1)}, bf16[6,64,2048]{2,1,0:T(8,128)(2,1)}, u32[]{:S(2)}) copy-start(bf16[6,64,2048]{2,1,0:T(8,128)(2,1)} %param.18) | copy-start | bytes 4718596
  284.4 7.3 slice-start
  284.4 7.3 slice-start.1
  288.2 3.5 copy-start.17
  297.9 10.9 copy-start.27
  308.8 8.6 copy-start.29
  317.4 8.6 copy-start.32
  317.4 8.7 copy-start.31
  326.0 3.1 copy-start.30
  326.7 2.9 copy-start.28
  329.0 1.4 copy-start.10
  329.1 2.4 copy-start.20
  329.1 2.3 copy-start.36
  329.1 2.3 copy-start.37
  334.4 3.4 copy-start.3
  337.7 3.4 copy-start.4
  756.9 1.8 copy-start.6
  761.4 2.6 copy-start.1
  784.2 15.2 %copy-start.11 = (bf16[6,64,2048]{2,1,0:T(8,128)(2,1)S(1)}, bf16[6,64,2048]{2,1,0:T(8,128)(2,1)}, u32[]{:S(2)}) copy-start(bf16[6,64,2048]{2,1,0:T(8,128)(2,1)} %param.17) | copy-start | bytes 4718596
  784.2 15.2 %copy-start.14 = (f32[384,2048]{1,0:T(8,128)S(1)}, f32[384,2048]{1,0:T(8,128)}, u32[]{:S(2)}) copy-start(f32[384,2048]{1,0:T(8,128)} %copy-done.13) | copy-start | bytes 9437188
  784.2 15.2 %copy-start.15 = (f32[384,2048]{1,0:T(8,128)S(1)}, f32[384,2048]{1,0:T(8,128)}, u32[]{:S(2)}) copy-start(f32[384,2048]{1,0:T(8,128)} %get-tuple-element.60) | copy-start | bytes 9437188
  799.4 3.9 copy-start.2
  1174.1 3.3 copy-start.5
  1177.3 1.0 copy-start.7
  1178.4 1.0 copy-start.8
